TPU v7x, 32 devices: a whole 2x2x4 slice. The times are simulated.
32 devices in a mesh: groups: 2 (over y), ctx: 4 (over z), heads: 4 (over x, core).
Axes of the slice: x: 2, y: 2, z: 4, core: 2. Of those that a mesh axis runs over, the one named last changes fastest.
Arguments:
- ssm_input: bfloat16 [2048, 8192], P(('groups', 'ctx'), 'heads'), parts along dimension 0, may hold values from -6 to 6
- decay_log: float32 [2048, 128], P(('groups', 'ctx'), 'heads'), parts along dimension 0
- state_write: bfloat16 [2048, 128], P(('groups', 'ctx')), parts along dimension 0, may hold values from -2 to 2
- state_read: bfloat16 [2048, 128], P(('groups', 'ctx')), parts along dimension 0, may hold values from -2 to 2
- skip_scale: float32 [128], P('heads'), may hold values from 0.5 to 3
- gate_input: bfloat16 [2048, 8192], P(('groups', 'ctx'), 'heads'), parts along dimension 0, may hold values from -6 to 6
- ssm_gain: float32 [8192], P('heads'), may hold values from 0.1 to 1.9
- out_weight: bfloat16 [8192, 4096], P('heads', 'ctx'), may hold values from -0.0625 to 0.0625
- residual_in: bfloat16 [2048, 4096], P(('groups', 'ctx'), 'heads'), parts along dimension 0, may hold values from -24 to 24
- moe_gain: float32 [4096], P('heads'), may hold values from 0.1 to 1.9
- down_latent: bfloat16 [4096, 1024], P('heads'), may hold values from -0.09375 to 0.09375
- expert_up: bfloat16 [8, 1024, 2688], P('ctx', None, 'heads'), may hold values from -0.1875 to 0.1875
- expert_down: bfloat16 [8, 2688, 1024], P('ctx', 'heads'), may hold values from -0.125 to 0.125
- up_latent: bfloat16 [1024, 4096], P(None, 'heads'), may hold values from -0.1875 to 0.1875
- expert_ids: int32 [2048, 22], P(('groups', 'ctx')), parts along dimension 0, may hold values from 0 to 511, as said below
- combine_fixed: int32 [2048, 22], P(('groups', 'ctx')), parts along dimension 0, may hold values from 1 to 65535
Outputs:
- layer_out: bfloat16 [2048, 4096], P(('groups', 'ctx'), 'heads'), parts along dimension 0
There are 2 independent parts, one for each index of `groups`. A program takes and returns all parts, laid end to end along the dimension named above; an argument that names none is the same for every part. Nothing has to cross between parts.
Inputs may be any that keep to these rules, and one draw needn't show every extreme that they name: `expert_ids`: each row names 22 different experts. No expert below 8 is named by more than 16 of the 256 tokens of one block, and in every block some expert below 8 is named by exactly 16 of them.
All inputs are finite; a program needn't handle non-finite values.
Results may differ from a plain program's by a relative error of at most 0.014.
Values may be sent and summed in bfloat16 or wider, within the bound.
A program may use at most 128 MiB of HBM per device.

v0:
```python
import functools

import jax
import jax.numpy as jnp
from jax import lax
from jax.experimental import pallas as pl
from jax.experimental.pallas import tpu as pltpu
from jax.sharding import PartitionSpec as P

D = 4096
GRP = 1024
LAT = 1024
CAP = 16


epsilon = 1e-05


MESH = pl.DeviceIdType.MESH
BF = jnp.bfloat16
F32 = jnp.float32


def vmem(count=1):
    return [pl.BlockSpec(memory_space=pltpu.VMEM)] * count


def greet(device):
    pl.semaphore_signal(
        pltpu.get_barrier_semaphore(), inc=1, device_id=device, device_id_type=MESH
    )


def greeted(count):
    pl.semaphore_wait(pltpu.get_barrier_semaphore(), count)


def one_if(condition):
    return jnp.where(condition, 1, 0)


def remote(src, dst, send, recv, device):
    return pltpu.make_async_remote_copy(
        src_ref=src, dst_ref=dst, send_sem=send, recv_sem=recv, device_id=device, device_id_type=MESH
    )


def pair_wide(first, second, width):
    lane = lax.broadcasted_iota(jnp.int32, (first.shape[0], 2 * width), 1)
    return jnp.where(lane < width, first, second)


def scan_kernel(width, x_ref, col_ref, row_ref, write_ref, read_ref, skip_ref, mixed_ref, state_ref, decay_ref, inter):
    rows = x_ref.shape[0]
    band = rows // 2
    t = lax.broadcasted_iota(jnp.int32, (rows, rows), 0)
    s = lax.broadcasted_iota(jnp.int32, (rows, rows), 1)
    causal = t >= s

    @pl.when(pl.program_id(0) == 0)
    def _():
        product = lax.dot_general(
            read_ref[...], write_ref[...], (((1,), (1,)), ((), ())), preferred_element_type=F32
        )
        inter[...] = jnp.where(causal, product, 0.0)

    x = x_ref[...]
    outs, tails, ends = [], [], []
    for j in range(2):
        col = col_ref[0, :, j : j + 1]
        row = row_ref[0, j : j + 1, :]
        last = row_ref[0, j : j + 1, rows - 1 : rows]
        lane = x[:, j * width : (j + 1) * width]
        bands = []
        for lo in range(0, rows, band):
            hi = lo + band
            spread = jnp.where(causal[lo:hi, lo:hi], col[lo:hi] - row[:, lo:hi], 0.0)
            if lo:
                spread = jnp.concatenate([col[lo:hi] - row[:, :lo], spread], axis=1)
            mixing = (jnp.exp(-spread) * inter[lo:hi, :hi]).astype(BF)
            bands.append(jnp.dot(mixing, lane[:hi], preferred_element_type=F32))
        outs.append(jnp.concatenate(bands, axis=0))
        tails.append(jnp.exp(col - last))
        ends.append(jnp.exp(-last))
    wide = x.astype(F32)
    mixed_ref[...] = jnp.concatenate(outs, axis=1) + skip_ref[...] * wide
    scaled = (wide * pair_wide(tails[0], tails[1], width)).astype(BF)
    state_ref[...] = lax.dot_general(
        write_ref[...], scaled, (((0,), (0,)), ((), ())), preferred_element_type=F32
    )
    decay_ref[...] = pair_wide(ends[0], ends[1], width)


def chain_kernel(n, chunks, state_ref, decay_ref, prior_ref, landed, outgoing, send_sem, recv_sem):
    me = lax.axis_index("ctx")
    size = state_ref.shape[1] // chunks
    has_prev, has_next = me > 0, me < n - 1
    prev, after = jnp.maximum(me - 1, 0), jnp.minimum(me + 1, n - 1)
    pl.when(has_prev)(lambda: greet({"ctx": prev}))
    pl.when(has_next)(lambda: greet({"ctx": after}))
    greeted(one_if(has_prev) + one_if(has_next))

    def copy(k):
        return remote(
            outgoing.at[k], landed.at[k], send_sem.at[k], recv_sem.at[k], {"ctx": after}
        )

    for k in range(chunks):
        part = pl.ds(k * size, size)

        @pl.when(me == 0)
        def _():
            prior_ref[:, part] = jnp.zeros((state_ref.shape[0], size), BF)

            if n > 1:
                outgoing[k] = state_ref[:, part].astype(BF)

        @pl.when(has_prev)
        def _():
            copy(k).wait_recv()
            came = landed[k]
            prior_ref[:, part] = came
            outgoing[k] = (came.astype(F32) * decay_ref[:, part] + state_ref[:, part]).astype(BF)

        pl.when(has_next)(lambda: copy(k).start())
    for k in range(chunks):
        pl.when(has_next)(lambda: copy(k).wait_send())


def gate_kernel(width, mixed_ref, prior_ref, col_ref, read_ref, gate_ref, gain_ref, normed_ref, gated):
    rows = mixed_ref.shape[0]
    pairs = col_ref.shape[0]
    squares = jnp.zeros((rows, 2 * width), F32)
    for p in range(pairs):
        part = slice(p * 2 * width, (p + 1) * 2 * width)
        reach = pair_wide(
            jnp.exp(-col_ref[p, :, 0:1]), jnp.exp(-col_ref[p, :, 1:2]), width
        )
        carried = jnp.dot(read_ref[...], prior_ref[:, part], preferred_element_type=F32) * reach
        gate = gate_ref[:, part].astype(F32)
        value = (mixed_ref[:, part] + carried) * (gate / (1.0 + jnp.exp(-gate)))
        gated[:, part] = value
        squares = squares + value * value
    scale = lax.rsqrt(jnp.sum(squares, axis=1, keepdims=True) / (pairs * 2 * width) + epsilon)
    normed_ref[...] = (gated[...] * scale * gain_ref[...]).astype(BF)


def project_kernel(
    n, heads, normed_ref, weight_ref, out_ref,
    blocks, parts, gathered, summed, final,
    up_send, up_recv, down_send, down_recv, part_send, part_recv, sum_send, sum_recv,
):
    me, head = lax.axis_index("ctx"), lax.axis_index("heads")
    share = n // heads
    column_head = me // share
    rows, width = normed_ref.shape[0], weight_ref.shape[1]
    prev, after = (me + n - 1) % n, (me + 1) % n
    half = rows // 2

    def holder(j):
        return head * share + j, column_head

    def other(j):
        ctx, side = holder(j)
        return jnp.logical_or(ctx != me, side != head)

    greet({"ctx": prev})
    greet({"ctx": after})
    for k in range(1, heads):
        greet({"heads": (head + k) % heads})
    count = heads + 1
    for j in range(share):
        ctx, side = holder(j)
        pl.when(other(j))(lambda: greet({"ctx": ctx, "heads": side}))
        count = count + one_if(other(j))
    greeted(count)

    def up_rows(s):
        return pl.ds(0, half if 2 * s == n else rows)

    def down_rows(s):
        return pl.ds(half, half) if 2 * s == n else pl.ds(0, rows)

    def upward(s, src, block):
        part = up_rows(s)
        return remote(
            src.at[part], blocks.at[block, part], up_send.at[s], up_recv.at[s], {"ctx": after}
        )

    def downward(s, src, block):
        part = down_rows(s)
        return remote(
            src.at[part], blocks.at[block, part], down_send.at[s], down_recv.at[s], {"ctx": prev}
        )

    def part_copy(b, target):
        return remote(
            parts.at[b], gathered.at[b % share, head], part_send.at[b],
            part_recv.at[b % share, head], {"heads": target},
        )

    def multiply(b, src, start, size):
        step = min(width, 256)
        for lo in range(0, width, step):
            parts[b, start : start + size, lo : lo + step] = jnp.dot(
                src[start : start + size, :], weight_ref[:, lo : lo + step],
                preferred_element_type=F32,
            ).astype(BF)

    def deliver(b):
        target = b // share
        pl.when(target != head)(lambda: part_copy(b, target).start())

    reach = n // 2
    upward(1, normed_ref, me).start()
    downward(1, normed_ref, me).start()
    multiply(me, normed_ref, 0, rows)
    deliver(me)
    for s in range(1, reach + 1):
        low, high = (me + n - s) % n, (me + s) % n
        upward(s, normed_ref, low).wait_recv()
        if s < reach:
            upward(s + 1, blocks.at[low], low).start()
        downward(s, normed_ref, high).wait_recv()
        if s < reach:
            downward(s + 1, blocks.at[high], high).start()
            multiply(low, blocks.at[low], 0, rows)
            deliver(low)
            multiply(high, blocks.at[high], 0, rows)
        else:
            multiply(high, blocks.at[high], 0, rows)
        deliver(high)

    def sum_copy(j):
        ctx, side = holder(j)
        return remote(
            summed.at[j], final.at[me % share], sum_send.at[j], sum_recv.at[me % share],
            {"ctx": ctx, "heads": side},
        )

    for j in range(share):
        mine = head * share + j
        total = parts[mine].astype(F32)
        for k in range(1, heads):
            source = (head + k) % heads
            remote(
                parts.at[mine], gathered.at[j, source], part_send.at[mine],
                part_recv.at[j, source], {"heads": source},
            ).wait_recv()
            total = total + gathered[j, source].astype(F32)
        summed[j] = total.astype(BF)
        pl.when(other(j))(lambda: sum_copy(j).start())

    for i in range(share):
        ctx, side = holder(i)
        here = slice(i * width, (i + 1) * width)

        @pl.when(other(i))
        def _():
            remote(
                summed.at[i], final.at[i], sum_send.at[i], sum_recv.at[i],
                {"ctx": ctx, "heads": side},
            ).wait_recv()
            out_ref[:, here] = final[i].astype(F32)

        @pl.when(jnp.logical_not(other(i)))
        def _():
            out_ref[:, here] = summed[me % share].astype(F32)

    for s in range(1, reach + 1):
        upward(s, normed_ref, me).wait_send()
        downward(s, normed_ref, me).wait_send()
    for b in range(n):
        pl.when(b // share != head)(lambda: part_copy(b, b // share).wait_send())
    for j in range(share):
        pl.when(other(j))(lambda: sum_copy(j).wait_send())


def slots_kernel(
    n, heads, width, features, src_ref, out_ref,
    first, middle, second, third,
    first_send, first_recv, second_send, second_recv, third_send, third_recv,
):
    me, head = lax.axis_index("ctx"), lax.axis_index("heads")

    for k in range(1, heads):
        greet({"heads": (head + k) % heads})
    for k in range(1, n):
        greet({"ctx": (me + k) % n})
    greeted(heads + n - 2)

    def first_copy(k):
        to = (head + k) % heads
        return remote(
            src_ref.at[to], first.at[k], first_send.at[k], first_recv.at[k], {"heads": to}
        )

    def second_copy(k):
        to = (me + k) % n
        return remote(
            middle.at[to], second.at[me], second_send.at[k], second_recv.at[k], {"ctx": to}
        )

    def third_copy(k):
        to = (head + k) % heads
        return remote(second, third.at[k], third_send.at[k], third_recv.at[k], {"heads": to})

    for k in range(1, heads):
        first_copy(k).start()
    total = src_ref[head].astype(F32)
    for k in range(1, heads):
        first_copy(k).wait_recv()
        total = total + first[k].astype(F32)
    if src_ref.shape[-1] > width:
        power = total[:, :, width : width + 1]
        total = total[:, :, :width] * lax.rsqrt(power / features + epsilon)
    middle[...] = total.astype(BF)
    for k in range(1, n):
        second_copy(k).start()
    second[me] = middle[me]
    for k in range(1, n):
        second_copy(k).wait_recv()
    for k in range(1, heads):
        third_copy(k).start()
    out_ref[head] = second[...]
    for k in range(1, heads):
        third_copy(k).wait_recv()
        out_ref[(head + heads - k) % heads] = third[k]
    for k in range(1, heads):
        first_copy(k).wait_send()
        third_copy(k).wait_send()
    for k in range(1, n):
        second_copy(k).wait_send()


def reaching(collective_id):
    return pltpu.CompilerParams(
        collective_id=collective_id, has_side_effects=True, vmem_limit_bytes=48 * 1024 * 1024
    )


def dma(*shape):
    return pltpu.SemaphoreType.DMA(shape)


def through_slots(pieces, width, features, collective_id):
    heads, n, rows, wide = pieces.shape
    return pl.pallas_call(
        functools.partial(slots_kernel, n, heads, width, features),
        out_shape=jax.ShapeDtypeStruct((heads, n, rows, width), BF),
        in_specs=vmem(),
        out_specs=vmem()[0],
        scratch_shapes=[
            pltpu.VMEM((heads, n, rows, wide), BF),
            pltpu.VMEM((n, rows, width), BF),
            pltpu.VMEM((n, rows, width), BF),
            pltpu.VMEM((heads, n, rows, width), BF),
            dma(heads), dma(heads), dma(n), dma(n), dma(heads), dma(heads),
        ],
        compiler_params=reaching(collective_id),
    )(pieces)


def mixer(ssm_input, decay_log, state_write, state_read, skip_scale, gate_input, ssm_gain):
    n = lax.axis_size("ctx")
    rows, columns = ssm_input.shape
    head_count = decay_log.shape[1]
    width = columns // head_count
    pairs, states = head_count // 2, state_write.shape[1]
    cumulative = jnp.cumsum(decay_log, axis=0)
    by_row = cumulative.T.reshape(pairs, 2, rows)
    by_col = by_row.transpose(0, 2, 1)
    skip = jnp.repeat(skip_scale, width).reshape(1, columns)
    span = 2 * width
    whole = lambda p: (0, 0)
    mixed, state, decay = pl.pallas_call(
        functools.partial(scan_kernel, width),
        grid=(pairs,),
        out_shape=(
            jax.ShapeDtypeStruct((rows, columns), F32),
            jax.ShapeDtypeStruct((states, columns), F32),
            jax.ShapeDtypeStruct((1, columns), F32),
        ),
        in_specs=[
            pl.BlockSpec((rows, span), lambda p: (0, p)),
            pl.BlockSpec((1, rows, 2), lambda p: (p, 0, 0)),
            pl.BlockSpec((1, 2, rows), lambda p: (p, 0, 0)),
            pl.BlockSpec((rows, states), whole),
            pl.BlockSpec((rows, states), whole),
            pl.BlockSpec((1, span), lambda p: (0, p)),
        ],
        out_specs=(
            pl.BlockSpec((rows, span), lambda p: (0, p)),
            pl.BlockSpec((states, span), lambda p: (0, p)),
            pl.BlockSpec((1, span), lambda p: (0, p)),
        ),
        scratch_shapes=[pltpu.VMEM((rows, rows), F32)],
    )(ssm_input, by_col, by_row, state_write, state_read, skip)
    chunks = 8
    prior = pl.pallas_call(
        functools.partial(chain_kernel, n, chunks),
        out_shape=jax.ShapeDtypeStruct((states, columns), BF),
        in_specs=vmem(2),
        out_specs=vmem()[0],
        scratch_shapes=[
            pltpu.VMEM((chunks, states, columns // chunks), BF),
            pltpu.VMEM((chunks, states, columns // chunks), BF),
            dma(chunks),
            dma(chunks),
        ],
        compiler_params=reaching(1),
    )(state, decay)
    group_pairs = GRP // span
    at = lambda g: (0, g)
    return pl.pallas_call(
        functools.partial(gate_kernel, width),
        grid=(columns // GRP,),
        out_shape=jax.ShapeDtypeStruct((rows, columns), BF),
        in_specs=[
            pl.BlockSpec((rows, GRP), at),
            pl.BlockSpec((states, GRP), at),
            pl.BlockSpec((group_pairs, rows, 2), lambda g: (g, 0, 0)),
            pl.BlockSpec((rows, states), whole),
            pl.BlockSpec((rows, GRP), at),
            pl.BlockSpec((1, GRP), at),
        ],
        out_specs=pl.BlockSpec((rows, GRP), at),
        scratch_shapes=[pltpu.VMEM((rows, GRP), F32)],
    )(mixed, prior, by_col, state_read, gate_input, ssm_gain.reshape(1, columns))


def project(normed, weight):
    n, heads = lax.axis_size("ctx"), lax.axis_size("heads")
    rows, width = normed.shape[0], weight.shape[1]
    share = n // heads
    block = (rows, width)
    return pl.pallas_call(
        functools.partial(project_kernel, n, heads),
        out_shape=jax.ShapeDtypeStruct((rows, share * width), F32),
        in_specs=vmem(2),
        out_specs=vmem()[0],
        scratch_shapes=[
            pltpu.VMEM((n,) + normed.shape, BF),
            pltpu.VMEM((n,) + block, BF),
            pltpu.VMEM((share, heads) + block, BF),
            pltpu.VMEM((share,) + block, BF),
            pltpu.VMEM((share,) + block, BF),
            dma(n), dma(n), dma(n), dma(n), dma(n), dma(share, heads), dma(share), dma(share),
        ],
        compiler_params=reaching(2),
    )(normed, weight)


def local(
    ssm_input,
    decay_log,
    state_write,
    state_read,
    skip_scale,
    gate_input,
    ssm_gain,
    out_weight,
    residual_in,
    moe_gain,
    down_latent,
    expert_up,
    expert_down,
    up_latent,
    expert_ids,
    combine_fixed,
):
    row_count = ssm_input.shape[0]
    n, heads = lax.axis_size("ctx"), lax.axis_size("heads")
    features = residual_in.shape[1] * heads
    latent_width = down_latent.shape[1]
    piece = latent_width // heads
    experts_here = expert_up.shape[0]
    wave_size = experts_here * n
    slot_rows = experts_here * CAP

    matches = expert_ids[:, :, None] == jnp.arange(wave_size)[None, None, :]
    chosen = jnp.any(matches, axis=1).astype(jnp.int32)
    weight_fixed = jnp.sum(jnp.where(matches, combine_fixed[:, :, None], 0), axis=1)
    slot_index = jnp.cumsum(chosen, axis=0) - 1
    placed = (chosen[:, :, None] == 1) & (slot_index[:, :, None] == jnp.arange(CAP)[None, None, :])
    route_weight = (weight_fixed.astype(F32) / 65536.0).astype(BF)
    combine_table = jnp.where(placed, route_weight[:, :, None], jnp.zeros((), BF)).reshape(
        row_count, wave_size * CAP
    )
    placed = placed.astype(BF).reshape(row_count, wave_size * CAP)

    normed = mixer(
        ssm_input, decay_log, state_write, state_read, skip_scale, gate_input, ssm_gain
    )
    residual = residual_in.astype(F32) + project(normed, out_weight)
    scaled = (residual * moe_gain).astype(BF)
    latent_part = jnp.dot(scaled, down_latent, preferred_element_type=F32).astype(BF)
    squares = jnp.sum(residual * residual, axis=1).astype(BF)
    side = jnp.concatenate(
        [latent_part, jnp.broadcast_to(squares[:, None], (row_count, 128))], axis=1
    )
    slots = lax.dot_general(
        placed, side, (((0,), (0,)), ((), ())), preferred_element_type=F32
    ).astype(BF)
    slots = slots.reshape(n, slot_rows, latent_width + 128)
    pieces = jnp.stack(
        [
            jnp.concatenate(
                [slots[:, :, h * piece : (h + 1) * piece], slots[:, :, latent_width:]], axis=2
            )
            for h in range(heads)
        ]
    )
    incoming = through_slots(pieces, piece, features, 3)
    incoming = incoming.reshape(heads, n, experts_here, CAP, piece).transpose(2, 1, 3, 0, 4)
    incoming = incoming.reshape(experts_here, n * CAP, latent_width)
    hidden = jnp.einsum("esl,elf->esf", incoming, expert_up, preferred_element_type=F32)
    hidden = (jnp.maximum(hidden, 0.0) ** 2).astype(BF)
    expert_out = jnp.einsum("esf,efl->esl", hidden, expert_down, preferred_element_type=F32)
    expert_out = expert_out.astype(BF).reshape(experts_here, n, CAP, heads, piece)
    expert_out = expert_out.transpose(3, 1, 0, 2, 4).reshape(heads, n, slot_rows, piece)
    returned = through_slots(expert_out, piece, features, 4)
    returned = returned.transpose(1, 2, 0, 3).reshape(wave_size * CAP, latent_width)
    combined = jnp.dot(combine_table, returned, preferred_element_type=F32)
    moe_out = jnp.dot(combined.astype(BF), up_latent, preferred_element_type=F32)
    return (residual + moe_out).astype(BF)


def solution(mesh):
    placed = (
        P(("groups", "ctx"), "heads"),
        P(("groups", "ctx"), "heads"),
        P(("groups", "ctx"), None),
        P(("groups", "ctx"), None),
        P("heads"),
        P(("groups", "ctx"), "heads"),
        P("heads"),
        P("heads", "ctx"),
        P(("groups", "ctx"), "heads"),
        P("heads"),
        P("heads", None),
        P("ctx", None, "heads"),
        P("ctx", "heads", None),
        P(None, "heads"),
        P(("groups", "ctx"), None),
        P(("groups", "ctx"), None),
    )
    return jax.shard_map(
        local, mesh=mesh, in_specs=placed, out_specs=P(("groups", "ctx"), "heads"), check_vma=False
    )
```

profile of v0, /device:TPU:1, one launch (start us, length us, event | category | flops | bytes accessed | tf_op | source)
XLA Modules:
  0.0 200.9 jit_solution(17681774374773401351)
XLA Ops:
  0.0 0.9 copy_bitcast_fusion.1
  0.9 0.6 reduce-window.14
  1.5 0.2 slice_reduce_fusion
  1.7 0.1 broadcast_add_fusion
  1.9 2.0 %copy.32 = f32[16,2,256]{1,2,0:T(8,128)} copy(f32[16,2,256]{2,1,0:T(2,128)S(1)} %reduce_window_sum.30.row_ref) | data formatting | bytes 65536 | tf_op jit(solution)/shard_map/reduce_window_sum
  4.0 0.7 reshape_reshape.3.skip_ref
  4.6 13.2 %shard_map.154 = (f32[256,2048]{1,0:T(8,128)}, f32[128,2048]{1,0:T(8,128)}, f32[1,2048]{1,0:T(1,128)}) custom-call(bf16[256,2048]{1,0:T(8,128)(2,1)} %x_ref.1, f32[16,256,2]{2,1,0:T(8,128)} %bitcast.54, f32[16,2,256]{2,1,0:T(2,128)} %copy-done.8, bf16[256,128]{1,0:T(8,128)(2,1)} %write_ref.1, bf16[256,128]{1,0:T(8,128)(2,1)} %read_ref.3, ...), custom_call_target="tpu_custom_call" | custom-call | tf_op jit(solution)/shard_map/pallas_call | solution.py:376
  17.8 1.2 copy-done.4
  19.1 0.7 copy-done.5
  19.8 12.9 %shard_map.155.prior_ref = bf16[128,2048]{1,0:T(8,128)(2,1)S(1)} custom-call(f32[128,2048]{1,0:T(8,128)S(1)} %copy-done.4, f32[1,2048]{1,0:T(1,128)S(1)} %copy-done.5), custom_call_target="tpu_custom_call" | custom-call | tf_op jit(solution)/shard_map/pallas_call | solution.py:400
  32.7 0.8 copy-done.3
  33.4 4.8 %shard_map.156.normed_ref = bf16[256,2048]{1,0:T(8,128)(2,1)} custom-call(f32[256,2048]{1,0:T(8,128)} %get-tuple-element.8.mixed_ref, bf16[128,2048]{1,0:T(8,128)(2,1)} %copy-done.3, f32[16,256,2]{2,1,0:T(8,128)} %bitcast.55, bf16[256,128]{1,0:T(8,128)(2,1)} %read_ref.3, bf16[256,2048]{1,0:T(8,128)(2,1)} %gate_ref.1, f32[1,2048]{1,0:T(1,128)} %bitcast.63), custom_call_target="tpu_custom_call" | custom-call | tf_op jit(solution)/shard_map/pallas_call | solution.py:415
  38.3 1.2 copy-done.2
  39.5 98.5 %shard_map.157 = f32[256,1024]{1,0:T(8,128)S(1)} custom-call(bf16[256,2048]{1,0:T(8,128)(2,1)S(1)} %copy-done.2, bf16[2048,1024]{1,0:T(8,128)(2,1)} %weight_ref.1), custom_call_target="tpu_custom_call" | custom-call | tf_op jit(solution)/shard_map/pallas_call | solution.py:437
  138.1 1.5 convolution_convert_fusion.1
  139.6 0.2 multiply_reduce_fusion
  139.8 0.1 broadcast_in_dim.46
  140.0 0.6 reduce-window.16
  140.5 0.2 slice_reduce_fusion.1
  140.8 0.1 add_bitcast_fusion
  140.9 0.1 eq.66
  141.0 0.1 fusion.11
  141.1 1.3 convolution_convert_fusion
  142.5 31.2 %shard_map.158 = bf16[4,4,32,256]{3,2,1,0:T(8,128)(2,1)S(1)} custom-call(bf16[4,4,32,384]{3,2,1,0:T(8,128)(2,1)S(1)} %pad_maximum_fusion.src_ref), custom_call_target="tpu_custom_call" | custom-call | tf_op jit(solution)/shard_map/pallas_call | solution.py:348
  173.8 0.9 copy.40
  174.7 1.1 reshape.116
  175.8 3.9 %convolution_convert_fusion.3 = bf16[2,64,1024]{2,1,0:T(8,128)(2,1)} fusion(bf16[2,672,1024]{2,1,0:T(8,128)(2,1)S(1)} %copy-done, bf16[2,64,1024]{2,1,0:T(8,128)(2,1)S(1)} %reshape.116, bf16[2,1024,672]{1,2,0:T(8,128)(2,1)} %param.27), kind=kOutput, calls=%fused_computation.5 | convolution fusion | flops 352710656 | bytes 6029312 | tf_op jit(solution)/shard_map/esf,efl->esl/dot_general | solution.py:519
  179.7 1.1 reshape.117
  180.9 15.5 %shard_map.159 = bf16[4,4,32,256]{3,2,1,0:T(8,128)(2,1)S(1)} custom-call(bf16[4,4,32,256]{3,2,1,0:T(8,128)(2,1)S(1)} %bitcast.52), custom_call_target="tpu_custom_call" | custom-call | tf_op jit(solution)/shard_map/pallas_call | solution.py:348
  196.4 0.2 copy.35
  196.7 0.7 fusion.10
  197.3 3.5 %fusion = bf16[256,1024]{1,0:T(8,128)(2,1)} fusion(bf16[1024,1024]{1,0:T(8,128)(2,1)} %param.29, bf16[256,128]{0,1:T(8,128)(2,1)} %bitcast.62, bf16[128,1024]{1,0:T(8,128)(2,1)S(1)} %bitcast.56, f32[256,1024]{1,0:T(8,128)} %copy-done.1, bf16[256,1024]{1,0:T(8,128)(2,1)S(1)} %copy-done.6), kind=kOutput, calls=%fused_computation.3 | convolution fusion | flops 605290496 | bytes 4521984 | tf_op jit(solution)/shard_map/dot_general | solution.py:525
  (42 shorter events, 0.6 us)
Async XLA Ops:
  0.0 175.8 %copy-start = (bf16[2,672,1024]{2,1,0:T(8,128)(2,1)S(1)}, bf16[2,672,1024]{2,1,0:T(8,128)(2,1)}, u32[]{:S(2)}) copy-start(bf16[2,672,1024]{2,1,0:T(8,128)(2,1)} %param.28) | copy-start | bytes 8257540
  0.0 3.9 %copy-start.13 = (f32[32]{0:T(128)S(1)}, f32[32]{0:T(128)}, u32[]{:S(2)}) copy-start(f32[32]{0:T(128)} %param.20) | copy-start | bytes 388
  1.9 2.8 %copy-start.8 = (f32[16,2,256]{2,1,0:T(2,128)}, f32[16,2,256]{2,1,0:T(2,128)S(1)}, u32[]{:S(2)}) copy-start(f32[16,2,256]{2,1,0:T(2,128)S(1)} %reduce_window_sum.30.row_ref) | copy-start | bytes 98308
  17.8 1.2 copy-start.4
  19.1 0.7 copy-start.5
  32.6 0.8 copy-start.3
  38.3 1.2 copy-start.2
  39.5 98.5 %copy-start.6 = (bf16[256,1024]{1,0:T(8,128)(2,1)S(1)}, bf16[256,1024]{1,0:T(8,128)(2,1)}, u32[]{:S(2)}) copy-start(bf16[256,1024]{1,0:T(8,128)(2,1)} %param.24) | copy-start | bytes 1572868
  39.5 98.5 %copy-start.7 = (bf16[1024,1024]{1,0:T(8,128)(2,1)S(1)}, bf16[1024,1024]{1,0:T(8,128)(2,1)}, u32[]{:S(2)}) copy-start(bf16[1024,1024]{1,0:T(8,128)(2,1)} %param.26) | copy-start | bytes 6291460
  39.5 98.5 %copy-start.12 = (f32[1024]{0:T(1024)S(1)}, f32[1024]{0:T(1024)}, u32[]{:S(2)}) copy-start(f32[1024]{0:T(1024)} %param.25) | copy-start | bytes 12292
  138.0 1.5 copy-start.1
  138.1 1.9 copy-start.9
  180.8 15.8 %copy-start.10 = (s32[256,22]{0,1:T(8,128)S(1)}, s32[256,22]{0,1:T(8,128)}, u32[]{:S(2)}) copy-start(s32[256,22]{0,1:T(8,128)} %param.30) | copy-start | bytes 67588
  180.9 15.8 %copy-start.11 = (s32[256,22]{0,1:T(8,128)S(1)}, s32[256,22]{0,1:T(8,128)}, u32[]{:S(2)}) copy-start(s32[256,22]{0,1:T(8,128)} %param.31) | copy-start | bytes 67588
where the time goes:
time: 202 us; the launch traced here: 201 us
  Pallas kernels  176 us (87%)
  local copies, waits for them, and re-layouts  11.8 us (6%)
  matrix products  10.2 us (5%)
  other arithmetic  2.54 us (1%)
    pallas_call x1, Pallas kernels, project(): pl.pallas_call(functools.partial(project_kernel, n, heads), out_shape=jax...  98.5 us
    pallas_call x2, Pallas kernels, through_slots(): pl.pallas_call(functools.partial(slots_kernel, n, heads, width, features)...  46.7 us
    pallas_call x1, Pallas kernels, mixer(): pl.pallas_call(functools.partial(scan_kernel, width), grid=(pairs,), out_...  13.2 us
    pallas_call x1, Pallas kernels, mixer(): pl.pallas_call(functools.partial(chain_kernel, n, chunks), out_shape=jax....  12.9 us
    pallas_call x1, Pallas kernels, mixer(): pl.pallas_call(functools.partial(gate_kernel, width), grid=(columns // GR...  4.85 us

commit v1 on v0

v1 whole, which is shorter than its diff:
```python
import functools

import jax
import jax.numpy as jnp
from jax import lax
from jax.experimental import pallas as pl
from jax.experimental.pallas import tpu as pltpu
from jax.sharding import PartitionSpec as P

D = 4096
GRP = 1024
LAT = 1024
CAP = 16


epsilon = 1e-05


MESH = pl.DeviceIdType.MESH
BF = jnp.bfloat16
F32 = jnp.float32


def vmem(count=1):
    return [pl.BlockSpec(memory_space=pltpu.VMEM)] * count


def greet(device):
    pl.semaphore_signal(
        pltpu.get_barrier_semaphore(), inc=1, device_id=device, device_id_type=MESH
    )


def greeted(count):
    pl.semaphore_wait(pltpu.get_barrier_semaphore(), count)


def one_if(condition):
    return jnp.where(condition, 1, 0)


def remote(src, dst, send, recv, device):
    return pltpu.make_async_remote_copy(
        src_ref=src, dst_ref=dst, send_sem=send, recv_sem=recv, device_id=device, device_id_type=MESH
    )


def pair_wide(first, second, width):
    lane = lax.broadcasted_iota(jnp.int32, (first.shape[0], 2 * width), 1)
    return jnp.where(lane < width, first, second)


def mixer_kernel(
    n, heads, width, piece, lag,
    x_hbm, gate_hbm, weight_hbm, resid_hbm, decay_ref, write_ref, read_ref, skip_ref, gain_ref,
    out_ref,
    x_ref, gate_ref, weight_ref, resid_ref, cum, cum_rows, skips, inter,
    mixed, state, ends, prior, outgoing, gated,
    blocks, acc, parts, core_in, chip_out, x_in, fin_out, final,
    load_sem, chain_send, chain_recv, up_send, up_recv, down_send, down_recv,
    core_send, core_recv, x_send, x_recv, fin_send, fin_recv,
):
    me, head = lax.axis_index("ctx"), lax.axis_index("heads")
    rows, columns = x_ref.shape
    span = 2 * width
    pairs = columns // span
    head_count = decay_ref.shape[1]
    out_width = weight_ref.shape[1]
    count = columns // piece
    share = n // heads
    cores = 2
    chips = heads // cores
    core, chip = head % cores, head // cores
    half, strip = out_width // cores, rows // chips
    has_prev, has_next = me > 0, me < n - 1
    prev, after = jnp.maximum(me - 1, 0), jnp.minimum(me + 1, n - 1)

    loads = [
        pltpu.make_async_copy(src, dst, load_sem.at[i])
        for i, (src, dst) in enumerate(
            [(x_hbm, x_ref), (gate_hbm, gate_ref), (weight_hbm, weight_ref), (resid_hbm, resid_ref)]
        )
    ]
    for load in loads:
        load.start()
    for i in range(n):
        for j in range(heads):
            if i or j:
                greet({"ctx": (me + i) % n, "heads": (head + j) % heads})

    t = lax.broadcasted_iota(jnp.int32, (rows, rows), 0)
    s = lax.broadcasted_iota(jnp.int32, (rows, rows), 1)
    lower = jnp.where(t >= s, 1.0, 0.0)
    cum[...] = jnp.zeros(cum.shape, F32)
    cum[:, :head_count] = jnp.dot(
        lower, decay_ref[...], precision=lax.Precision.HIGHEST, preferred_element_type=F32
    )
    cum_rows[...] = lax.dot_general(
        decay_ref[...], lower, (((0,), (1,)), ((), ())),
        precision=lax.Precision.HIGHEST, preferred_element_type=F32,
    )
    skips[...] = jnp.zeros(skips.shape, F32)
    skips[0:1, :head_count] = skip_ref[...]
    product = lax.dot_general(
        read_ref[...], write_ref[...], (((1,), (1,)), ((), ())), preferred_element_type=F32
    )
    inter[...] = jnp.where(t >= s, product, 0.0)
    greeted(n * heads - 1)
    loads[0].wait()

    def lanes(p):
        return pl.ds(pl.multiple_of(p * span, span), span)

    def shifted(ref, p):
        lane_count = ref.shape[1]
        return pltpu.roll(ref[...], (lane_count - 2 * p) % lane_count, 1)

    band = rows // 2
    causal = lax.broadcasted_iota(jnp.int32, (band, band), 0) >= lax.broadcasted_iota(
        jnp.int32, (band, band), 1
    )

    def scan(p):
        x = x_ref[:, lanes(p)]
        cols = shifted(cum, p)
        skip = shifted(skips, p)
        outs, tails, lasts = [], [], []
        for j in range(2):
            col = cols[:, j : j + 1]
            row = cum_rows[pl.ds(2 * p + j, 1), :]
            last = col[rows - 1 : rows, :]
            lane = x[:, j * width : (j + 1) * width]
            bands = []
            for lo in range(0, rows, band):
                hi = lo + band
                spread = jnp.where(causal, col[lo:hi] - row[:, lo:hi], 0.0)
                if lo:
                    spread = jnp.concatenate([col[lo:hi] - row[:, :lo], spread], axis=1)
                mixing = (jnp.exp(-spread) * inter[lo:hi, :hi]).astype(BF)
                bands.append(jnp.dot(mixing, lane[:hi], preferred_element_type=F32))
            outs.append(jnp.concatenate(bands, axis=0))
            tails.append(jnp.exp(col - last))
            lasts.append(jnp.exp(-last))
        wide = x.astype(F32)
        direct = pair_wide(skip[0:1, 0:1], skip[0:1, 1:2], width) * wide
        mixed[p] = jnp.concatenate(outs, axis=1) + direct
        scaled = (wide * pair_wide(tails[0], tails[1], width)).astype(BF)
        state[p] = lax.dot_general(
            write_ref[...], scaled, (((0,), (0,)), ((), ())), preferred_element_type=F32
        )
        ends[p] = pair_wide(lasts[0], lasts[1], width)

    def chain_copy(q):
        return remote(
            outgoing.at[q], prior.at[q], chain_send.at[q], chain_recv.at[q], {"ctx": after}
        )

    def chain(q):
        @pl.when(me == 0)
        def _():
            prior[q] = jnp.zeros(prior.shape[1:], BF)
            outgoing[q] = state[q].astype(BF)

        @pl.when(has_prev)
        def _():
            chain_copy(q).wait_recv()
            outgoing[q] = (prior[q].astype(F32) * ends[q] + state[q]).astype(BF)

        pl.when(has_next)(lambda: chain_copy(q).start())

    def advance(i, carry):
        pl.when(i < pairs)(lambda: scan(i))
        q = i - lag * me
        pl.when(jnp.logical_and(q >= 0, q < pairs))(lambda: chain(q))
        return carry

    lax.fori_loop(0, pairs + lag * (n - 1), advance, 0)

    def upward(b, p):
        spot = blocks.at[b, p]
        return remote(spot, spot, up_send.at[b, p], up_recv.at[b, p], {"ctx": after})

    def downward(b, p):
        spot = blocks.at[b, p]
        return remote(spot, spot, down_send.at[b, p], down_recv.at[b, p], {"ctx": prev})

    group_pairs = GRP // span
    group_pieces = GRP // piece
    piece_pairs = piece // span
    loads[1].wait()

    def gate(g, carry):
        squares = jnp.zeros((rows, span), F32)
        for i in range(group_pairs):
            p = g * group_pairs + i
            cols = shifted(cum, p)
            reach = jnp.exp(-pair_wide(cols[:, 0:1], cols[:, 1:2], width))
            carried = jnp.dot(read_ref[...], prior[p], preferred_element_type=F32) * reach
            gating = gate_ref[:, lanes(p)].astype(F32)
            value = (mixed[p] + carried) * (gating / (1.0 + jnp.exp(-gating)))
            gated[i] = value
            squares = squares + value * value
        scale = lax.rsqrt(jnp.sum(squares, axis=1, keepdims=True) / GRP + epsilon)
        for i in range(group_pairs):
            p = g * group_pairs + i
            value = (gated[i] * scale * gain_ref[:, lanes(p)]).astype(BF)
            lo = (i % piece_pairs) * span
            blocks[me, g * group_pieces + i // piece_pairs, :, lo : lo + span] = value
        for k in range(group_pieces):
            p = g * group_pieces + k
            pl.when(has_next)(lambda: upward(me, p).start())
            pl.when(has_prev)(lambda: downward(me, p).start())
        return carry

    lax.fori_loop(0, columns // GRP, gate, 0)
    loads[2].wait()

    def multiply(slot, b, p):
        step = min(out_width, 256)
        fed = blocks[b, p]
        for lo in range(0, out_width, step):
            held = acc[slot, :, lo : lo + step]
            part = weight_ref[pl.ds(pl.multiple_of(p * piece, piece), piece), lo : lo + step]
            acc[slot, :, lo : lo + step] = jnp.where(p == 0, 0.0, held) + jnp.dot(
                fed, part, preferred_element_type=F32
            )

    def core_copy(b):
        return remote(
            parts.at[b, 1 - core], core_in.at[b], core_send.at[b], core_recv.at[b],
            {"heads": head + 1 - 2 * core},
        )

    def round_partial(b, slot):
        for k in range(cores):
            parts[b, k] = acc[slot, :, k * half : (k + 1) * half].astype(BF)
        core_copy(b).start()

    def chip_copy(b, k):
        to = (chip + k) % chips
        return remote(
            chip_out.at[b, to], x_in.at[b, k], x_send.at[b, k], x_recv.at[b, k],
            {"heads": to * cores + core},
        )

    def sum_cores(b):
        core_copy(b).wait_recv()
        for k in range(chips):
            part = slice(k * strip, (k + 1) * strip)
            both = parts[b, core, part].astype(F32) + core_in[b, part].astype(F32)
            chip_out[b, k] = both.astype(BF)
        for k in range(1, chips):
            chip_copy(b, k).start()

    def local_final(b):
        return jnp.logical_and(b == me, head == me // share)

    def final_copy(b):
        return remote(
            fin_out.at[b], final.at[me % share, head], fin_send.at[b],
            fin_recv.at[me % share, head], {"ctx": b, "heads": me // share},
        )

    def sum_chips(b):
        part = pl.ds(pl.multiple_of(chip * strip, strip), strip)
        total = parts[b, core, part].astype(F32) + core_in[b, part].astype(F32)
        for k in range(1, chips):
            chip_copy(b, k).wait_recv()
            total = total + x_in[b, k].astype(F32)
        fin_out[b] = total.astype(BF)

        @pl.when(local_final(b))
        def _():
            final[me % share, head] = total.astype(BF)

        pl.when(jnp.logical_not(local_final(b)))(lambda: final_copy(b).start())

    def own(p, carry):
        multiply(0, me, p)
        return carry

    lax.fori_loop(0, count, own, 0)
    round_partial(me, 0)

    def around(s, act):
        low, high = me - s, me + s
        pl.when(low >= 0)(lambda: act(jnp.maximum(low, 0), 0))

        @pl.when(jnp.logical_and(high < n, s > 0))
        def _():
            act(jnp.minimum(high, n - 1), 1)

    def step(i, carry):
        s, p = 1 + i // count, i % count
        low, high = me - s, me + s
        low_spot, high_spot = jnp.maximum(low, 0), jnp.minimum(high, n - 1)

        @pl.when(low >= 0)
        def _():
            upward(low_spot, p).wait_recv()
            pl.when(has_next)(lambda: upward(low_spot, p).start())

        @pl.when(high < n)
        def _():
            downward(high_spot, p).wait_recv()
            pl.when(has_prev)(lambda: downward(high_spot, p).start())

        around(s, lambda b, slot: multiply(slot, b, p))
        pl.when(p == count - 1)(lambda: around(s, round_partial))
        pl.when(p == 0)(lambda: around(s - 1, lambda b, slot: sum_cores(b)))
        pl.when(p == min(1, count - 1))(lambda: around(s - 1, lambda b, slot: sum_chips(b)))
        return carry

    lax.fori_loop(0, (n - 1) * count, step, 0)
    around(n - 1, lambda b, slot: sum_cores(b))
    around(n - 1, lambda b, slot: sum_chips(b))
    loads[3].wait()

    for j in range(share):
        source = head * share + j
        for k in range(heads):
            here = jnp.logical_and(source == me, k == head)

            @pl.when(jnp.logical_not(here))
            def _():
                remote(
                    fin_out.at[0], final.at[j, k], fin_send.at[0], fin_recv.at[j, k],
                    {"ctx": source, "heads": k},
                ).wait_recv()

            part = slice((k // cores) * strip, (k // cores + 1) * strip)
            lo = j * out_width + (k % cores) * half
            out_ref[part, lo : lo + half] = (
                resid_ref[part, lo : lo + half].astype(F32) + final[j, k].astype(F32)
            )

    for q in range(pairs):
        pl.when(has_next)(lambda: chain_copy(q).wait_send())
    for b in range(n):
        for p in range(count):
            pl.when(jnp.logical_and(has_next, b <= me))(lambda: upward(b, p).wait_send())
            pl.when(jnp.logical_and(has_prev, b >= me))(lambda: downward(b, p).wait_send())
        core_copy(b).wait_send()
        for k in range(1, chips):
            chip_copy(b, k).wait_send()
        pl.when(jnp.logical_not(local_final(b)))(lambda: final_copy(b).wait_send())


def slots_kernel(
    n, heads, width, features, src_ref, out_ref,
    first, middle, second, third,
    first_send, first_recv, second_send, second_recv, third_send, third_recv,
):
    me, head = lax.axis_index("ctx"), lax.axis_index("heads")

    for k in range(1, heads):
        greet({"heads": (head + k) % heads})
    for k in range(1, n):
        greet({"ctx": (me + k) % n})
    greeted(heads + n - 2)

    def first_copy(k):
        to = (head + k) % heads
        return remote(
            src_ref.at[to], first.at[k], first_send.at[k], first_recv.at[k], {"heads": to}
        )

    def second_copy(k):
        to = (me + k) % n
        return remote(
            middle.at[to], second.at[me], second_send.at[k], second_recv.at[k], {"ctx": to}
        )

    def third_copy(k):
        to = (head + k) % heads
        return remote(second, third.at[k], third_send.at[k], third_recv.at[k], {"heads": to})

    for k in range(1, heads):
        first_copy(k).start()
    total = src_ref[head].astype(F32)
    for k in range(1, heads):
        first_copy(k).wait_recv()
        total = total + first[k].astype(F32)
    if src_ref.shape[-1] > width:
        power = total[:, :, width : width + 1]
        total = total[:, :, :width] * lax.rsqrt(power / features + epsilon)
    middle[...] = total.astype(BF)
    for k in range(1, n):
        second_copy(k).start()
    second[me] = middle[me]
    for k in range(1, n):
        second_copy(k).wait_recv()
    for k in range(1, heads):
        third_copy(k).start()
    out_ref[head] = second[...]
    for k in range(1, heads):
        third_copy(k).wait_recv()
        out_ref[(head + heads - k) % heads] = third[k]
    for k in range(1, heads):
        first_copy(k).wait_send()
        third_copy(k).wait_send()
    for k in range(1, n):
        second_copy(k).wait_send()


def reaching(collective_id):
    return pltpu.CompilerParams(
        collective_id=collective_id, has_side_effects=True, vmem_limit_bytes=48 * 1024 * 1024
    )


def dma(*shape):
    return pltpu.SemaphoreType.DMA(shape)


def through_slots(pieces, width, features, collective_id):
    heads, n, rows, wide = pieces.shape
    return pl.pallas_call(
        functools.partial(slots_kernel, n, heads, width, features),
        out_shape=jax.ShapeDtypeStruct((heads, n, rows, width), BF),
        in_specs=vmem(),
        out_specs=vmem()[0],
        scratch_shapes=[
            pltpu.VMEM((heads, n, rows, wide), BF),
            pltpu.VMEM((n, rows, width), BF),
            pltpu.VMEM((n, rows, width), BF),
            pltpu.VMEM((heads, n, rows, width), BF),
            dma(heads), dma(heads), dma(n), dma(n), dma(heads), dma(heads),
        ],
        compiler_params=reaching(collective_id),
    )(pieces)


def mixer(
    ssm_input, decay_log, state_write, state_read, skip_scale, gate_input, ssm_gain, weight, residual_in
):
    n, heads = lax.axis_size("ctx"), lax.axis_size("heads")
    rows, columns = ssm_input.shape
    head_count = decay_log.shape[1]
    width = columns // head_count
    states = state_write.shape[1]
    span = 2 * width
    pairs = columns // span
    piece = GRP // 2
    count = columns // piece
    out_width = weight.shape[1]
    share = n // heads
    chips = heads // 2
    half, strip = out_width // 2, rows // chips
    lane_count = -(-head_count // 128) * 128
    block = (rows, out_width)
    anywhere = pl.BlockSpec(memory_space=pl.ANY)
    return pl.pallas_call(
        functools.partial(mixer_kernel, n, heads, width, piece, 3),
        out_shape=jax.ShapeDtypeStruct((rows, share * out_width), F32),
        in_specs=[anywhere] * 4 + vmem(5),
        out_specs=vmem()[0],
        scratch_shapes=[
            pltpu.VMEM((rows, columns), BF),
            pltpu.VMEM((rows, columns), BF),
            pltpu.VMEM(weight.shape, BF),
            pltpu.VMEM(residual_in.shape, BF),
            pltpu.VMEM((rows, lane_count), F32),
            pltpu.VMEM((head_count, rows), F32),
            pltpu.VMEM((8, lane_count), F32),
            pltpu.VMEM((rows, rows), F32),
            pltpu.VMEM((pairs, rows, span), F32),
            pltpu.VMEM((pairs, states, span), F32),
            pltpu.VMEM((pairs, 1, span), F32),
            pltpu.VMEM((pairs, states, span), BF),
            pltpu.VMEM((pairs, states, span), BF),
            pltpu.VMEM((GRP // span, rows, span), F32),
            pltpu.VMEM((n, count, rows, piece), BF),
            pltpu.VMEM((2,) + block, F32),
            pltpu.VMEM((n, 2, rows, half), BF),
            pltpu.VMEM((n, rows, half), BF),
            pltpu.VMEM((n, chips, strip, half), BF),
            pltpu.VMEM((n, chips, strip, half), BF),
            pltpu.VMEM((n, strip, half), BF),
            pltpu.VMEM((share, heads, strip, half), BF),
            dma(4), dma(pairs), dma(pairs),
            dma(n, count), dma(n, count), dma(n, count), dma(n, count),
            dma(n), dma(n), dma(n, chips), dma(n, chips), dma(n), dma(share, heads),
        ],
        compiler_params=reaching(1),
    )(
        ssm_input, gate_input, weight, residual_in, decay_log, state_write, state_read,
        skip_scale.reshape(1, head_count), ssm_gain.reshape(1, columns),
    )


def local(
    ssm_input,
    decay_log,
    state_write,
    state_read,
    skip_scale,
    gate_input,
    ssm_gain,
    out_weight,
    residual_in,
    moe_gain,
    down_latent,
    expert_up,
    expert_down,
    up_latent,
    expert_ids,
    combine_fixed,
):
    row_count = ssm_input.shape[0]
    n, heads = lax.axis_size("ctx"), lax.axis_size("heads")
    features = residual_in.shape[1] * heads
    latent_width = down_latent.shape[1]
    piece = latent_width // heads
    experts_here = expert_up.shape[0]
    wave_size = experts_here * n
    slot_rows = experts_here * CAP

    matches = expert_ids[:, :, None] == jnp.arange(wave_size)[None, None, :]
    chosen = jnp.any(matches, axis=1).astype(jnp.int32)
    weight_fixed = jnp.sum(jnp.where(matches, combine_fixed[:, :, None], 0), axis=1)
    slot_index = jnp.cumsum(chosen, axis=0) - 1
    placed = (chosen[:, :, None] == 1) & (slot_index[:, :, None] == jnp.arange(CAP)[None, None, :])
    route_weight = (weight_fixed.astype(F32) / 65536.0).astype(BF)
    combine_table = jnp.where(placed, route_weight[:, :, None], jnp.zeros((), BF)).reshape(
        row_count, wave_size * CAP
    )
    placed = placed.astype(BF).reshape(row_count, wave_size * CAP)

    residual = mixer(
        ssm_input, decay_log, state_write, state_read, skip_scale, gate_input, ssm_gain,
        out_weight, residual_in,
    )
    scaled = (residual * moe_gain).astype(BF)
    latent_part = jnp.dot(scaled, down_latent, preferred_element_type=F32).astype(BF)
    squares = jnp.sum(residual * residual, axis=1).astype(BF)
    side = jnp.concatenate(
        [latent_part, jnp.broadcast_to(squares[:, None], (row_count, 128))], axis=1
    )
    slots = lax.dot_general(
        placed, side, (((0,), (0,)), ((), ())), preferred_element_type=F32
    ).astype(BF)
    slots = slots.reshape(n, slot_rows, latent_width + 128)
    pieces = jnp.stack(
        [
            jnp.concatenate(
                [slots[:, :, h * piece : (h + 1) * piece], slots[:, :, latent_width:]], axis=2
            )
            for h in range(heads)
        ]
    )
    incoming = through_slots(pieces, piece, features, 3)
    incoming = incoming.reshape(heads, n, experts_here, CAP, piece).transpose(2, 1, 3, 0, 4)
    incoming = incoming.reshape(experts_here, n * CAP, latent_width)
    hidden = jnp.einsum("esl,elf->esf", incoming, expert_up, preferred_element_type=F32)
    hidden = (jnp.maximum(hidden, 0.0) ** 2).astype(BF)
    expert_out = jnp.einsum("esf,efl->esl", hidden, expert_down, preferred_element_type=F32)
    expert_out = expert_out.astype(BF).reshape(experts_here, n, CAP, heads, piece)
    expert_out = expert_out.transpose(3, 1, 0, 2, 4).reshape(heads, n, slot_rows, piece)
    returned = through_slots(expert_out, piece, features, 4)
    returned = returned.transpose(1, 2, 0, 3).reshape(wave_size * CAP, latent_width)
    combined = jnp.dot(combine_table, returned, preferred_element_type=F32)
    moe_out = jnp.dot(combined.astype(BF), up_latent, preferred_element_type=F32)
    return (residual + moe_out).astype(BF)


def solution(mesh):
    placed = (
        P(("groups", "ctx"), "heads"),
        P(("groups", "ctx"), "heads"),
        P(("groups", "ctx"), None),
        P(("groups", "ctx"), None),
        P("heads"),
        P(("groups", "ctx"), "heads"),
        P("heads"),
        P("heads", "ctx"),
        P(("groups", "ctx"), "heads"),
        P("heads"),
        P("heads", None),
        P("ctx", None, "heads"),
        P("ctx", "heads", None),
        P(None, "heads"),
        P(("groups", "ctx"), None),
        P(("groups", "ctx"), None),
    )
    return jax.shard_map(
        local, mesh=mesh, in_specs=placed, out_specs=P(("groups", "ctx"), "heads"), check_vma=False
    )
```

time: 202 us -> 158 us (0.78)
  Pallas kernels: 176 us -> 139 us
  local copies, waits for them, and re-layouts: 11.8 us -> 8.76 us
  matrix products: 10.2 us -> 7.67 us
    pallas_call x4 -> x1, Pallas kernels: 129 us -> 106 us  [mixer(): pl.pallas_call(functools.partial(mixer_kernel, n, heads, width, piece, 3)...]
    pallas_call x2, Pallas kernels: 46.7 us -> 33.4 us  [through_slots(): pl.pallas_call(functools.partial(slots_kernel, n, heads, width, features)...]
    unnamed x29 -> x28, local copies, waits for them, and re-layouts: 4.01 us -> 7.54 us
    another operation x7 -> x1, local copies, waits for them, and re-layouts: 2.99 us -> 0.01 us
where the time goes in v1:
time: 158 us
  Pallas kernels  139 us (88%)
  local copies, waits for them, and re-layouts  8.76 us (6%)
  matrix products  7.67 us (5%)
  other arithmetic  2.06 us (1%)
    pallas_call x1, Pallas kernels, mixer(): pl.pallas_call(functools.partial(mixer_kernel, n, heads, width, piece, 3)...  106 us
    pallas_call x2, Pallas kernels, through_slots(): pl.pallas_call(functools.partial(slots_kernel, n, heads, width, features)...  33.4 us
    unnamed x28, local copies, waits for them, and re-layouts  7.54 us
    dot_general x1, matrix products, local(): jnp.dot(combined.astype(BF), up_latent, preferred_element_type=F32)  3.51 us
    dot_general x1, matrix products, local(): jnp.einsum('esf,efl->esl', hidden, expert_down, preferred_element_type=F32)  3.19 us

profile of v1, /device:TPU:1, one launch (start us, length us, event | category | flops | bytes accessed | tf_op | source)
XLA Modules:
  0.0 157.9 jit_solution(15866357942804750390)
XLA Ops:
  0.0 0.9 fusion.8
  0.9 0.6 reduce-window.6
  1.5 0.2 slice_reduce_fusion
  1.8 0.1 add_bitcast_fusion
  1.9 0.1 eq.66
  1.9 0.1 fusion.11
  2.1 0.9 copy.27.decay_ref
  2.9 0.0 copy-start.2
  2.9 1.2 copy-done.2
  4.1 1.2 copy-done.3
  5.4 1.0 copy-done.4
  6.4 0.8 copy-done.5
  7.2 0.8 copy-done.6
  8.1 0.7 copy-done.7
  8.8 0.7 copy-done.8
  9.4 105.8 %shard_map.154 = f32[256,1024]{1,0:T(8,128)S(1)} custom-call(bf16[256,2048]{1,0:T(8,128)(2,1)S(1)} %copy-done.2, bf16[256,2048]{1,0:T(8,128)(2,1)S(1)} %copy-done.3, bf16[2048,1024]{1,0:T(8,128)(2,1)} %weight_hbm.1, bf16[256,1024]{1,0:T(8,128)(2,1)S(1)} %copy-done.4, f32[256,32]{1,0:T(8,128)S(1)} %copy.27.decay_ref, bf16[256,128]{1,0:T(8,128)(2,1)S(1)} %copy-done.5, ...), custom_call_target="tpu_custom_call" | custom-call | tf_op jit(solution)/shard_map/pallas_call | solution.py:453
  115.3 0.7 convolution_convert_fusion.1
  116.0 0.1 multiply_reduce_fusion
  116.2 0.1 copy-done.1
  116.3 0.1 broadcast_in_dim.42
  116.4 0.3 convolution_convert_fusion
  116.7 0.1 pad_maximum_fusion.src_ref
  116.8 18.0 %shard_map.155 = bf16[4,4,32,256]{3,2,1,0:T(8,128)(2,1)S(1)} custom-call(bf16[4,4,32,384]{3,2,1,0:T(8,128)(2,1)S(1)} %pad_maximum_fusion.src_ref), custom_call_target="tpu_custom_call" | custom-call | tf_op jit(solution)/shard_map/pallas_call | solution.py:418
  134.8 0.2 copy.33
  135.0 0.2 reshape.105
  135.2 3.2 %convolution_convert_fusion.3 = bf16[2,64,1024]{2,1,0:T(8,128)(2,1)S(1)} fusion(bf16[2,672,1024]{2,1,0:T(8,128)(2,1)S(1)} %copy-done, bf16[2,64,1024]{2,1,0:T(8,128)(2,1)S(1)} %reshape.105, bf16[2,1024,672]{1,2,0:T(8,128)(2,1)} %param.27), kind=kOutput, calls=%fused_computation.5 | convolution fusion | flops 352710656 | bytes 6029312 | tf_op jit(solution)/shard_map/esf,efl->esl/dot_general | solution.py:557
  138.4 0.0 copy-start.10
  138.4 0.0 copy-start.11
  138.4 0.2 reshape.106
  138.7 15.4 %shard_map.156 = bf16[4,4,32,256]{3,2,1,0:T(8,128)(2,1)S(1)} custom-call(bf16[4,4,32,256]{3,2,1,0:T(8,128)(2,1)S(1)} %bitcast.46), custom_call_target="tpu_custom_call" | custom-call | tf_op jit(solution)/shard_map/pallas_call | solution.py:418
  154.1 0.2 copy.30
  154.4 3.5 %fusion = bf16[256,1024]{1,0:T(8,128)(2,1)} fusion(f32[256,1024]{1,0:T(8,128)} %copy-done.1, bf16[1024,1024]{1,0:T(8,128)(2,1)} %param.29, bf16[256,128]{0,1:T(8,128)(2,1)S(1)} %bitcast.56, bf16[128,1024]{1,0:T(8,128)(2,1)S(1)} %bitcast.52), kind=kOutput, calls=%fused_computation.3 | convolution fusion | flops 604766208 | bytes 3997696 | tf_op jit(solution)/shard_map/dot_general | solution.py:563
  (27 shorter events, 0.3 us)
Async XLA Ops:
  0.0 135.2 %copy-start = (bf16[2,672,1024]{2,1,0:T(8,128)(2,1)S(1)}, bf16[2,672,1024]{2,1,0:T(8,128)(2,1)}, u32[]{:S(2)}) copy-start(bf16[2,672,1024]{2,1,0:T(8,128)(2,1)} %param.28) | copy-start | bytes 8257540
  2.9 1.2 copy-start.2
  4.1 1.2 copy-start.3
  5.4 1.0 copy-start.4
  6.4 0.8 copy-start.5
  7.2 0.8 copy-start.6
  8.1 0.7 copy-start.7
  8.8 0.7 copy-start.8
  9.4 105.8 %copy-start.9 = (bf16[1024,1024]{1,0:T(8,128)(2,1)S(1)}, bf16[1024,1024]{1,0:T(8,128)(2,1)}, u32[]{:S(2)}) copy-start(bf16[1024,1024]{1,0:T(8,128)(2,1)} %param.26) | copy-start | bytes 6291460
  9.4 105.8 %copy-start.12 = (f32[1024]{0:T(1024)S(1)}, f32[1024]{0:T(1024)}, u32[]{:S(2)}) copy-start(f32[1024]{0:T(1024)} %param.25) | copy-start | bytes 12292
  115.3 1.0 copy-start.1
  138.4 15.9 %copy-start.10 = (s32[256,22]{0,1:T(8,128)S(1)}, s32[256,22]{0,1:T(8,128)}, u32[]{:S(2)}) copy-start(s32[256,22]{0,1:T(8,128)} %param.30) | copy-start | bytes 67588
  138.4 15.9 %copy-start.11 = (s32[256,22]{0,1:T(8,128)S(1)}, s32[256,22]{0,1:T(8,128)}, u32[]{:S(2)}) copy-start(s32[256,22]{0,1:T(8,128)} %param.31) | copy-start | bytes 67588

commit v2 on v1

--- a/solution.py
+++ b/solution.py
@@ -11,6 +11,7 @@
 GRP = 1024
 LAT = 1024
 CAP = 16
+LENT_NUM, LENT_DEN = 3, 8
 
 
 epsilon = 1e-05
@@ -51,20 +52,21 @@
 
 
 def mixer_kernel(
-    n, heads, width, piece, lag,
-    x_hbm, gate_hbm, weight_hbm, resid_hbm, decay_ref, write_ref, read_ref, skip_ref, gain_ref,
+    n, heads, width, piece, lag, lent,
+    x_hbm, write_hbm, read_hbm, decay_hbm, skip_hbm, weight_hbm, gate_hbm, gain_hbm, resid_hbm,
     out_ref,
-    x_ref, gate_ref, weight_ref, resid_ref, cum, cum_rows, skips, inter,
+    x_ref, write_ref, read_ref, decay_ref, skip_ref, weight_ref, gate_ref, gain_ref, resid_ref,
+    cum, cum_rows, skips, inter,
     mixed, state, ends, prior, outgoing, gated,
-    blocks, acc, parts, core_in, chip_out, x_in, fin_out, final,
+    blocks, acc, parts, core_in, chip_out, x_in, fin_out, final, borrowed, strips,
     load_sem, chain_send, chain_recv, up_send, up_recv, down_send, down_recv,
-    core_send, core_recv, x_send, x_recv, fin_send, fin_recv,
+    core_send, core_recv, x_send, x_recv, fin_send, fin_recv, lend_send, lend_recv, strip_recv,
 ):
     me, head = lax.axis_index("ctx"), lax.axis_index("heads")
     rows, columns = x_ref.shape
     span = 2 * width
     pairs = columns // span
-    head_count = decay_ref.shape[1]
+    head_count = decay_ref.shape[0]
     out_width = weight_ref.shape[1]
     count = columns // piece
     share = n // heads
@@ -74,11 +76,20 @@
     half, strip = out_width // cores, rows // chips
     has_prev, has_next = me > 0, me < n - 1
     prev, after = jnp.maximum(me - 1, 0), jnp.minimum(me + 1, n - 1)
+    keep = count - lent
+    at_end = jnp.logical_or(me == 0, me == n - 1)
+    beside = jnp.logical_or(me == 1, me == n - 2)
+    end_here = jnp.where(me == 1, 0, n - 1)
+    beside_here = jnp.where(me == 0, 1, n - 2)
 
     loads = [
         pltpu.make_async_copy(src, dst, load_sem.at[i])
         for i, (src, dst) in enumerate(
-            [(x_hbm, x_ref), (gate_hbm, gate_ref), (weight_hbm, weight_ref), (resid_hbm, resid_ref)]
+            [
+                (x_hbm, x_ref), (write_hbm, write_ref), (read_hbm, read_ref), (decay_hbm, decay_ref),
+                (skip_hbm, skip_ref), (weight_hbm, weight_ref), (gate_hbm, gate_ref),
+                (gain_hbm, gain_ref), (resid_hbm, resid_ref),
+            ]
         )
     ]
     for load in loads:
@@ -92,11 +103,14 @@
     s = lax.broadcasted_iota(jnp.int32, (rows, rows), 1)
     lower = jnp.where(t >= s, 1.0, 0.0)
     cum[...] = jnp.zeros(cum.shape, F32)
-    cum[:, :head_count] = jnp.dot(
-        lower, decay_ref[...], precision=lax.Precision.HIGHEST, preferred_element_type=F32
+    for load in loads[:5]:
+        load.wait()
+    cum[:, :head_count] = lax.dot_general(
+        lower, decay_ref[...], (((1,), (1,)), ((), ())),
+        precision=lax.Precision.HIGHEST, preferred_element_type=F32,
     )
     cum_rows[...] = lax.dot_general(
-        decay_ref[...], lower, (((0,), (1,)), ((), ())),
+        decay_ref[...], lower, (((1,), (1,)), ((), ())),
         precision=lax.Precision.HIGHEST, preferred_element_type=F32,
     )
     skips[...] = jnp.zeros(skips.shape, F32)
@@ -106,7 +120,18 @@
     )
     inter[...] = jnp.where(t >= s, product, 0.0)
     greeted(n * heads - 1)
-    loads[0].wait()
+
+    def lend():
+        return remote(
+            weight_ref.at[pl.ds(keep * piece, lent * piece)], borrowed, lend_send.at[0],
+            lend_recv.at[0], {"ctx": beside_here},
+        )
+
+    @pl.when(me == n - 1)
+    def _():
+        loads[5].wait()
+        if lent:
+            lend().start()
 
     def lanes(p):
         return pl.ds(pl.multiple_of(p * span, span), span)
@@ -184,10 +209,26 @@
         spot = blocks.at[b, p]
         return remote(spot, spot, down_send.at[b, p], down_recv.at[b, p], {"ctx": prev})
 
+    @pl.when(me < n - 1)
+    def _():
+        loads[5].wait()
+        if lent:
+            pl.when(me == 0)(lambda: lend().start())
+
+    def goes_up(p):
+        return jnp.logical_and(has_next, jnp.logical_or(p < keep, me + 1 < n - 1))
+
+    def goes_down(p):
+        return jnp.logical_and(has_prev, jnp.logical_or(p < keep, me > 1))
+
+    def needed(p):
+        return jnp.logical_or(p < keep, jnp.logical_not(at_end))
+
     group_pairs = GRP // span
     group_pieces = GRP // piece
     piece_pairs = piece // span
-    loads[1].wait()
+    loads[6].wait()
+    loads[7].wait()
 
     def gate(g, carry):
         squares = jnp.zeros((rows, span), F32)
@@ -208,12 +249,11 @@
             blocks[me, g * group_pieces + i // piece_pairs, :, lo : lo + span] = value
         for k in range(group_pieces):
             p = g * group_pieces + k
-            pl.when(has_next)(lambda: upward(me, p).start())
-            pl.when(has_prev)(lambda: downward(me, p).start())
+            pl.when(goes_up(p))(lambda: upward(me, p).start())
+            pl.when(goes_down(p))(lambda: downward(me, p).start())
         return carry
 
     lax.fori_loop(0, columns // GRP, gate, 0)
-    loads[2].wait()
 
     def multiply(slot, b, p):
         step = min(out_width, 256)
@@ -225,55 +265,103 @@
                 fed, part, preferred_element_type=F32
             )
 
-    def core_copy(b):
+    def core_copy(b, kind):
         return remote(
-            parts.at[b, 1 - core], core_in.at[b], core_send.at[b], core_recv.at[b],
-            {"heads": head + 1 - 2 * core},
-        )
-
-    def round_partial(b, slot):
+            parts.at[kind, b, 1 - core], core_in.at[kind, b], core_send.at[kind, b],
+            core_recv.at[kind, b], {"heads": head + 1 - 2 * core},
+        )
+
+    def round_partial(b, slot, kind=0):
         for k in range(cores):
-            parts[b, k] = acc[slot, :, k * half : (k + 1) * half].astype(BF)
-        core_copy(b).start()
-
-    def chip_copy(b, k):
+            parts[kind, b, k] = acc[slot, :, k * half : (k + 1) * half].astype(BF)
+        core_copy(b, kind).start()
+
+    def chip_copy(b, k, kind):
         to = (chip + k) % chips
         return remote(
-            chip_out.at[b, to], x_in.at[b, k], x_send.at[b, k], x_recv.at[b, k],
-            {"heads": to * cores + core},
-        )
-
-    def sum_cores(b):
-        core_copy(b).wait_recv()
+            chip_out.at[kind, b, to], x_in.at[kind, b, k], x_send.at[kind, b, k],
+            x_recv.at[kind, b, k], {"heads": to * cores + core},
+        )
+
+    def sum_cores(b, kind=0):
+        core_copy(b, kind).wait_recv()
         for k in range(chips):
             part = slice(k * strip, (k + 1) * strip)
-            both = parts[b, core, part].astype(F32) + core_in[b, part].astype(F32)
-            chip_out[b, k] = both.astype(BF)
+            both = parts[kind, b, core, part].astype(F32) + core_in[kind, b, part].astype(F32)
+            chip_out[kind, b, k] = both.astype(BF)
         for k in range(1, chips):
-            chip_copy(b, k).start()
-
-    def local_final(b):
-        return jnp.logical_and(b == me, head == me // share)
-
-    def final_copy(b):
+            chip_copy(b, k, kind).start()
+
+    def local_final(b, column):
+        return jnp.logical_and(b == me, head == column // share)
+
+    def final_copy(b, column, kind):
         return remote(
-            fin_out.at[b], final.at[me % share, head], fin_send.at[b],
-            fin_recv.at[me % share, head], {"ctx": b, "heads": me // share},
+            fin_out.at[kind, b], final.at[column % share, head], fin_send.at[kind, b],
+            fin_recv.at[column % share, head], {"ctx": b, "heads": column // share},
+        )
+
+    def strip_copy(b):
+        return remote(
+            fin_out.at[0, b], strips.at[b], fin_send.at[0, b], strip_recv.at[b],
+            {"ctx": beside_here},
+        )
+
+    def to_beside(b):
+        if not lent:
+            return False
+        return jnp.logical_and(at_end, b != me)
+
+    def strip_total(b, kind):
+        part = pl.ds(pl.multiple_of(chip * strip, strip), strip)
+        total = parts[kind, b, core, part].astype(F32) + core_in[kind, b, part].astype(F32)
+        for k in range(1, chips):
+            chip_copy(b, k, kind).wait_recv()
+            total = total + x_in[kind, b, k].astype(F32)
+        return total
+
+    def deliver(b, column, kind, total):
+        @pl.when(local_final(b, column))
+        def _():
+            final[column % share, head] = total.astype(BF)
+
+        pl.when(jnp.logical_not(local_final(b, column)))(
+            lambda: final_copy(b, column, kind).start()
         )
 
     def sum_chips(b):
-        part = pl.ds(pl.multiple_of(chip * strip, strip), strip)
-        total = parts[b, core, part].astype(F32) + core_in[b, part].astype(F32)
-        for k in range(1, chips):
-            chip_copy(b, k).wait_recv()
-            total = total + x_in[b, k].astype(F32)
-        fin_out[b] = total.astype(BF)
-
-        @pl.when(local_final(b))
+        total = strip_total(b, 0)
+        fin_out[0, b] = total.astype(BF)
+        if lent:
+            pl.when(to_beside(b))(lambda: strip_copy(b).start())
+            pl.when(jnp.logical_not(to_beside(b)))(lambda: deliver(b, me, 0, total))
+        else:
+            deliver(b, me, 0, total)
+
+    def helps(b):
+        return jnp.logical_and(beside, b != end_here)
+
+    def helping(b):
+        @pl.when(helps(b))
         def _():
-            final[me % share, head] = total.astype(BF)
-
-        pl.when(jnp.logical_not(local_final(b)))(lambda: final_copy(b).start())
+            step = min(out_width, 256)
+            for lo in range(0, out_width, step):
+                total = jnp.zeros((rows, step), F32)
+                for k in range(lent):
+                    part = borrowed[k * piece : (k + 1) * piece, lo : lo + step]
+                    total = total + jnp.dot(
+                        blocks[b, keep + k], part, preferred_element_type=F32
+                    )
+                acc[2, :, lo : lo + step] = total
+            round_partial(b, 2, 1)
+
+    def combine(b):
+        @pl.when(helps(b))
+        def _():
+            strip_copy(b).wait_recv()
+            total = strip_total(b, 1) + strips[b].astype(F32)
+            fin_out[1, b] = total.astype(BF)
+            deliver(b, end_here, 1, total)
 
     def own(p, carry):
         multiply(0, me, p)
@@ -289,42 +377,64 @@
         @pl.when(jnp.logical_and(high < n, s > 0))
         def _():
             act(jnp.minimum(high, n - 1), 1)
+
+    def both_sides(s, act):
+        around(s, lambda b, slot: act(b))
 
     def step(i, carry):
         s, p = 1 + i // count, i % count
         low, high = me - s, me + s
         low_spot, high_spot = jnp.maximum(low, 0), jnp.minimum(high, n - 1)
-
-        @pl.when(low >= 0)
+        wanted = needed(p)
+
+        @pl.when(jnp.logical_and(low >= 0, wanted))
         def _():
             upward(low_spot, p).wait_recv()
-            pl.when(has_next)(lambda: upward(low_spot, p).start())
-
-        @pl.when(high < n)
+            pl.when(goes_up(p))(lambda: upward(low_spot, p).start())
+
+        @pl.when(jnp.logical_and(high < n, wanted))
         def _():
             downward(high_spot, p).wait_recv()
-            pl.when(has_prev)(lambda: downward(high_spot, p).start())
-
-        around(s, lambda b, slot: multiply(slot, b, p))
-        pl.when(p == count - 1)(lambda: around(s, round_partial))
-        pl.when(p == 0)(lambda: around(s - 1, lambda b, slot: sum_cores(b)))
-        pl.when(p == min(1, count - 1))(lambda: around(s - 1, lambda b, slot: sum_chips(b)))
+            pl.when(goes_down(p))(lambda: downward(high_spot, p).start())
+
+        pl.when(wanted)(lambda: around(s, lambda b, slot: multiply(slot, b, p)))
+        last = jnp.where(at_end, keep - 1, count - 1)
+        pl.when(p == last)(lambda: around(s, round_partial))
+
+        def at(spot, act):
+            pl.when(p == min(spot, count - 1))(lambda: both_sides(s - 1, act))
+
+        at(0, sum_cores)
+        at(1, sum_chips)
+        if lent:
+            @pl.when(jnp.logical_and(i == 0, beside))
+            def _():
+                lend().wait_recv()
+
+            at(2, helping)
+            at(3, lambda b: pl.when(helps(b))(lambda: sum_cores(b, 1)))
         return carry
 
     lax.fori_loop(0, (n - 1) * count, step, 0)
-    around(n - 1, lambda b, slot: sum_cores(b))
-    around(n - 1, lambda b, slot: sum_chips(b))
-    loads[3].wait()
+    both_sides(n - 1, sum_cores)
+    both_sides(n - 1, sum_chips)
+    if lent:
+        for s in range(n - 1):
+            both_sides(s, combine)
+    loads[8].wait()
 
     for j in range(share):
         source = head * share + j
+        if lent:
+            outer = jnp.logical_and(source != me, jnp.logical_or(source == 0, source == n - 1))
+            source = jnp.where(outer, jnp.where(source == 0, 1, n - 2), source)
         for k in range(heads):
             here = jnp.logical_and(source == me, k == head)
 
             @pl.when(jnp.logical_not(here))
             def _():
                 remote(
-                    fin_out.at[0], final.at[j, k], fin_send.at[0], fin_recv.at[j, k],
+                    fin_out.at[0, 0], final.at[j, k], fin_send.at[0, 0], fin_recv.at[j, k],
                     {"ctx": source, "heads": k},
                 ).wait_recv()
 
@@ -338,12 +448,26 @@
         pl.when(has_next)(lambda: chain_copy(q).wait_send())
     for b in range(n):
         for p in range(count):
-            pl.when(jnp.logical_and(has_next, b <= me))(lambda: upward(b, p).wait_send())
-            pl.when(jnp.logical_and(has_prev, b >= me))(lambda: downward(b, p).wait_send())
-        core_copy(b).wait_send()
+            pl.when(jnp.logical_and(goes_up(p), b <= me))(lambda: upward(b, p).wait_send())
+            pl.when(jnp.logical_and(goes_down(p), b >= me))(lambda: downward(b, p).wait_send())
+        core_copy(b, 0).wait_send()
         for k in range(1, chips):
-            chip_copy(b, k).wait_send()
-        pl.when(jnp.logical_not(local_final(b)))(lambda: final_copy(b).wait_send())
+            chip_copy(b, k, 0).wait_send()
+        sent = jnp.logical_or(to_beside(b), jnp.logical_not(local_final(b, me)))
+        pl.when(sent)(lambda: final_copy(b, me, 0).wait_send())
+
+        if lent:
+            @pl.when(helps(b))
+            def _():
+                core_copy(b, 1).wait_send()
+                for k in range(1, chips):
+                    chip_copy(b, k, 1).wait_send()
+                pl.when(jnp.logical_not(local_final(b, end_here)))(
+                    lambda: final_copy(b, end_here, 1).wait_send()
+                )
+
+    if lent:
+        pl.when(at_end)(lambda: lend().wait_send())
 
 
 def slots_kernel(
@@ -441,8 +565,9 @@
     states = state_write.shape[1]
     span = 2 * width
     pairs = columns // span
-    piece = GRP // 2
+    piece = GRP // 4
     count = columns // piece
+    lent = LENT_NUM * count // LENT_DEN if n > 3 else 0
     out_width = weight.shape[1]
     share = n // heads
     chips = heads // 2
@@ -451,14 +576,19 @@
     block = (rows, out_width)
     anywhere = pl.BlockSpec(memory_space=pl.ANY)
     return pl.pallas_call(
-        functools.partial(mixer_kernel, n, heads, width, piece, 3),
+        functools.partial(mixer_kernel, n, heads, width, piece, 3, lent),
         out_shape=jax.ShapeDtypeStruct((rows, share * out_width), F32),
-        in_specs=[anywhere] * 4 + vmem(5),
+        in_specs=[anywhere] * 9,
         out_specs=vmem()[0],
         scratch_shapes=[
             pltpu.VMEM((rows, columns), BF),
+            pltpu.VMEM((rows, states), BF),
+            pltpu.VMEM((rows, states), BF),
+            pltpu.VMEM((head_count, rows), F32),
+            pltpu.VMEM((1, head_count), F32),
+            pltpu.VMEM(weight.shape, BF),
             pltpu.VMEM((rows, columns), BF),
-            pltpu.VMEM(weight.shape, BF),
+            pltpu.VMEM((1, columns), F32),
             pltpu.VMEM(residual_in.shape, BF),
             pltpu.VMEM((rows, lane_count), F32),
             pltpu.VMEM((head_count, rows), F32),
@@ -471,21 +601,24 @@
             pltpu.VMEM((pairs, states, span), BF),
             pltpu.VMEM((GRP // span, rows, span), F32),
             pltpu.VMEM((n, count, rows, piece), BF),
-            pltpu.VMEM((2,) + block, F32),
-            pltpu.VMEM((n, 2, rows, half), BF),
-            pltpu.VMEM((n, rows, half), BF),
-            pltpu.VMEM((n, chips, strip, half), BF),
-            pltpu.VMEM((n, chips, strip, half), BF),
+            pltpu.VMEM((3,) + block, F32),
+            pltpu.VMEM((2, n, 2, rows, half), BF),
+            pltpu.VMEM((2, n, rows, half), BF),
+            pltpu.VMEM((2, n, chips, strip, half), BF),
+            pltpu.VMEM((2, n, chips, strip, half), BF),
+            pltpu.VMEM((2, n, strip, half), BF),
+            pltpu.VMEM((share, heads, strip, half), BF),
+            pltpu.VMEM((max(lent, 1) * piece, out_width), BF),
             pltpu.VMEM((n, strip, half), BF),
-            pltpu.VMEM((share, heads, strip, half), BF),
-            dma(4), dma(pairs), dma(pairs),
+            dma(9), dma(pairs), dma(pairs),
             dma(n, count), dma(n, count), dma(n, count), dma(n, count),
-            dma(n), dma(n), dma(n, chips), dma(n, chips), dma(n), dma(share, heads),
+            dma(2, n), dma(2, n), dma(2, n, chips), dma(2, n, chips), dma(2, n), dma(share, heads),
+            dma(1), dma(1), dma(n),
         ],
         compiler_params=reaching(1),
     )(
-        ssm_input, gate_input, weight, residual_in, decay_log, state_write, state_read,
-        skip_scale.reshape(1, head_count), ssm_gain.reshape(1, columns),
+        ssm_input, state_write, state_read, decay_log.T, skip_scale.reshape(1, head_count), weight,
+        gate_input, ssm_gain.reshape(1, columns), residual_in,
     )
 
 

time: 158 us -> 165 us (1.044)
  Pallas kernels: 139 us -> 146 us
    pallas_call x1, Pallas kernels: 106 us -> 110 us  [mixer(): pl.pallas_call(functools.partial(mixer_kernel, n, heads, width, piece, 3,...]
    pallas_call x2, Pallas kernels: 33.4 us -> 35.7 us  [through_slots(): pl.pallas_call(functools.partial(slots_kernel, n, heads, width, features)...]
    unnamed x28 -> x29, local copies, waits for them, and re-layouts: 7.54 us -> 7.44 us
where the time goes in v2:
time: 165 us
  Pallas kernels  146 us (88%)
  local copies, waits for them, and re-layouts  8.66 us (5%)
  matrix products  7.67 us (5%)
  other arithmetic  2.06 us (1%)
    pallas_call x1, Pallas kernels, mixer(): pl.pallas_call(functools.partial(mixer_kernel, n, heads, width, piece, 3,...  110 us
    pallas_call x2, Pallas kernels, through_slots(): pl.pallas_call(functools.partial(slots_kernel, n, heads, width, features)...  35.7 us
    unnamed x29, local copies, waits for them, and re-layouts  7.44 us
    dot_general x1, matrix products, local(): jnp.dot(combined.astype(BF), up_latent, preferred_element_type=F32)  3.51 us

profile of v2, /device:TPU:1, one launch (start us, length us, event | category | flops | bytes accessed | tf_op | source)
XLA Modules:
  0.0 164.7 jit_solution(11974127594490631048)
XLA Ops:
  0.0 0.9 fusion.8
  0.9 0.6 reduce-window.6
  1.5 0.2 slice_reduce_fusion
  1.8 0.1 add_bitcast_fusion
  1.9 0.1 eq.66
  1.9 0.1 fusion.11
  2.1 0.0 copy-start.2
  2.1 1.2 copy-done.2
  3.3 1.2 copy-done.3
  4.5 1.0 copy-done.4
  5.5 0.8 copy-done.5
  6.4 0.8 copy-done.6
  7.2 0.8 copy-done.7
  8.0 0.7 copy-done.8
  8.7 0.7 copy-done.9
  9.3 110.4 %shard_map.154 = f32[256,1024]{1,0:T(8,128)S(1)} custom-call(bf16[256,2048]{1,0:T(8,128)(2,1)S(1)} %copy-done.2, bf16[256,128]{1,0:T(8,128)(2,1)S(1)} %copy-done.5, bf16[256,128]{1,0:T(8,128)(2,1)S(1)} %copy-done.6, f32[32,256]{1,0:T(8,128)S(1)} %bitcast.49, f32[1,32]{1,0:T(1,128)S(1)} %bitcast.51, bf16[2048,1024]{1,0:T(8,128)(2,1)} %weight_hbm.1, ...), custom_call_target="tpu_custom_call" | custom-call | tf_op jit(solution)/shard_map/pallas_call | solution.py:578
  119.7 0.7 convolution_convert_fusion.1
  120.5 0.1 multiply_reduce_fusion
  120.6 0.1 copy-done.1
  120.7 0.1 broadcast_in_dim.42
  120.8 0.3 convolution_convert_fusion
  121.2 0.1 pad_maximum_fusion.src_ref
  121.3 21.7 %shard_map.155 = bf16[4,4,32,256]{3,2,1,0:T(8,128)(2,1)S(1)} custom-call(bf16[4,4,32,384]{3,2,1,0:T(8,128)(2,1)S(1)} %pad_maximum_fusion.src_ref), custom_call_target="tpu_custom_call" | custom-call | tf_op jit(solution)/shard_map/pallas_call | solution.py:542
  143.0 0.2 copy.30
  143.2 0.2 reshape.105
  143.4 3.2 %convolution_convert_fusion.3 = bf16[2,64,1024]{2,1,0:T(8,128)(2,1)S(1)} fusion(bf16[2,672,1024]{2,1,0:T(8,128)(2,1)S(1)} %copy-done, bf16[2,64,1024]{2,1,0:T(8,128)(2,1)S(1)} %reshape.105, bf16[2,1024,672]{1,2,0:T(8,128)(2,1)} %param.27), kind=kOutput, calls=%fused_computation.5 | convolution fusion | flops 352710656 | bytes 6029312 | tf_op jit(solution)/shard_map/esf,efl->esl/dot_general | solution.py:690
  146.6 0.0 copy-start.11
  146.6 0.0 copy-start.12
  146.6 0.2 reshape.106
  146.8 14.0 %shard_map.156 = bf16[4,4,32,256]{3,2,1,0:T(8,128)(2,1)S(1)} custom-call(bf16[4,4,32,256]{3,2,1,0:T(8,128)(2,1)S(1)} %bitcast.47), custom_call_target="tpu_custom_call" | custom-call | tf_op jit(solution)/shard_map/pallas_call | solution.py:542
  160.8 0.2 copy.27
  161.2 3.5 %fusion = bf16[256,1024]{1,0:T(8,128)(2,1)} fusion(f32[256,1024]{1,0:T(8,128)} %copy-done.1, bf16[1024,1024]{1,0:T(8,128)(2,1)} %param.29, bf16[256,128]{0,1:T(8,128)(2,1)S(1)} %bitcast.58, bf16[128,1024]{1,0:T(8,128)(2,1)S(1)} %bitcast.54), kind=kOutput, calls=%fused_computation.3 | convolution fusion | flops 604766208 | bytes 3997696 | tf_op jit(solution)/shard_map/dot_general | solution.py:696
  (28 shorter events, 0.3 us)
Async XLA Ops:
  0.0 143.4 %copy-start = (bf16[2,672,1024]{2,1,0:T(8,128)(2,1)S(1)}, bf16[2,672,1024]{2,1,0:T(8,128)(2,1)}, u32[]{:S(2)}) copy-start(bf16[2,672,1024]{2,1,0:T(8,128)(2,1)} %param.28) | copy-start | bytes 8257540
  2.1 1.2 copy-start.2
  3.3 1.2 copy-start.3
  4.5 1.0 copy-start.4
  5.5 0.8 copy-start.5
  6.4 0.8 copy-start.6
  7.2 0.8 copy-start.7
  8.0 0.7 copy-start.8
  8.7 0.7 copy-start.9
  9.3 110.4 %copy-start.10 = (bf16[1024,1024]{1,0:T(8,128)(2,1)S(1)}, bf16[1024,1024]{1,0:T(8,128)(2,1)}, u32[]{:S(2)}) copy-start(bf16[1024,1024]{1,0:T(8,128)(2,1)} %param.26) | copy-start | bytes 6291460
  9.3 110.4 %copy-start.13 = (f32[1024]{0:T(1024)S(1)}, f32[1024]{0:T(1024)}, u32[]{:S(2)}) copy-start(f32[1024]{0:T(1024)} %param.25) | copy-start | bytes 12292
  119.7 1.0 copy-start.1
  146.6 14.5 %copy-start.11 = (s32[256,22]{0,1:T(8,128)S(1)}, s32[256,22]{0,1:T(8,128)}, u32[]{:S(2)}) copy-start(s32[256,22]{0,1:T(8,128)} %param.30) | copy-start | bytes 67588
  146.6 14.5 %copy-start.12 = (s32[256,22]{0,1:T(8,128)S(1)}, s32[256,22]{0,1:T(8,128)}, u32[]{:S(2)}) copy-start(s32[256,22]{0,1:T(8,128)} %param.31) | copy-start | bytes 67588

commit v3 on v2

--- a/solution.py
+++ b/solution.py
@@ -52,7 +52,7 @@
 
 
 def mixer_kernel(
-    n, heads, width, piece, lag, lent,
+    n, heads, groups, width, piece, lag, lent,
     x_hbm, write_hbm, read_hbm, decay_hbm, skip_hbm, weight_hbm, gate_hbm, gain_hbm, resid_hbm,
     out_ref,
     x_ref, write_ref, read_ref, decay_ref, skip_ref, weight_ref, gate_ref, gain_ref, resid_ref,
@@ -60,9 +60,9 @@
     mixed, state, ends, prior, outgoing, gated,
     blocks, acc, parts, core_in, chip_out, x_in, fin_out, final, borrowed, strips,
     load_sem, chain_send, chain_recv, up_send, up_recv, down_send, down_recv,
-    core_send, core_recv, x_send, x_recv, fin_send, fin_recv, lend_send, lend_recv, strip_recv,
+    core_send, core_recv, x_send, x_recv, fin_send, fin_recv, lend_send, lend_recv, spread_send, spread_recv, strip_recv,
 ):
-    me, head = lax.axis_index("ctx"), lax.axis_index("heads")
+    me, head, group = lax.axis_index("ctx"), lax.axis_index("heads"), lax.axis_index("groups")
     rows, columns = x_ref.shape
     span = 2 * width
     pairs = columns // span
@@ -98,6 +98,8 @@
         for j in range(heads):
             if i or j:
                 greet({"ctx": (me + i) % n, "heads": (head + j) % heads})
+    for i in range(1, groups):
+        greet({"groups": (group + i) % groups})
 
     t = lax.broadcasted_iota(jnp.int32, (rows, rows), 0)
     s = lax.broadcasted_iota(jnp.int32, (rows, rows), 1)
@@ -119,19 +121,30 @@
         read_ref[...], write_ref[...], (((1,), (1,)), ((), ())), preferred_element_type=F32
     )
     inter[...] = jnp.where(t >= s, product, 0.0)
-    greeted(n * heads - 1)
-
-    def lend():
-        return remote(
-            weight_ref.at[pl.ds(keep * piece, lent * piece)], borrowed, lend_send.at[0],
-            lend_recv.at[0], {"ctx": beside_here},
+    greeted(n * heads + groups - 2)
+
+    share_rows = piece // groups
+
+    def lend(k):
+        return remote(
+            weight_ref.at[pl.ds((keep + k) * piece + group * share_rows, share_rows)],
+            borrowed.at[pl.ds(k * piece + group * share_rows, share_rows)],
+            lend_send.at[k], lend_recv.at[k], {"ctx": beside_here},
+        )
+
+    def spread(k, i, back=False):
+        owner = (group + groups - i) % groups if back else group
+        part = borrowed.at[pl.ds(k * piece + owner * share_rows, share_rows)]
+        return remote(
+            part, part, spread_send.at[k, i], spread_recv.at[k, i],
+            {"groups": (group + i) % groups},
         )
 
     @pl.when(me == n - 1)
     def _():
         loads[5].wait()
-        if lent:
-            lend().start()
+        for k in range(lent):
+            lend(k).start()
 
     def lanes(p):
         return pl.ds(pl.multiple_of(p * span, span), span)
@@ -209,11 +222,7 @@
         spot = blocks.at[b, p]
         return remote(spot, spot, down_send.at[b, p], down_recv.at[b, p], {"ctx": prev})
 
-    @pl.when(me < n - 1)
-    def _():
-        loads[5].wait()
-        if lent:
-            pl.when(me == 0)(lambda: lend().start())
+    pl.when(me < n - 1)(lambda: loads[5].wait())
 
     def goes_up(p):
         return jnp.logical_and(has_next, jnp.logical_or(p < keep, me + 1 < n - 1))
@@ -254,6 +263,8 @@
         return carry
 
     lax.fori_loop(0, columns // GRP, gate, 0)
+    for k in range(lent):
+        pl.when(me == 0)(lambda: lend(k).start())
 
     def multiply(slot, b, p):
         step = min(out_width, 256)
@@ -406,13 +417,35 @@
 
         at(0, sum_cores)
         at(1, sum_chips)
+        def reduce_help(b):
+            pl.when(helps(b))(lambda: sum_cores(b, 1))
+
+        for k in range(lent):
+            @pl.when(jnp.logical_and(beside, i == (n - 3) * count + min(2 * (k + 1), count - 1)))
+            def _():
+                lend(k).wait_recv()
+                for g in range(1, groups):
+                    spread(k, g).start()
+
         if lent:
-            @pl.when(jnp.logical_and(i == 0, beside))
+            @pl.when(i == (n - 2) * count - 1)
             def _():
-                lend().wait_recv()
-
-            at(2, helping)
-            at(3, lambda b: pl.when(helps(b))(lambda: sum_cores(b, 1)))
+                @pl.when(beside)
+                def _():
+                    for k in range(lent):
+                        for g in range(1, groups):
+                            spread(k, g, True).wait_recv()
+
+                for r in range(n - 2):
+                    both_sides(r, helping)
+
+            @pl.when(i == (n - 2) * count)
+            def _():
+                both_sides(n - 2, helping)
+                for r in range(n - 2):
+                    both_sides(r, reduce_help)
+
+            pl.when(i == (n - 2) * count + 1)(lambda: both_sides(n - 2, reduce_help))
         return carry
 
     lax.fori_loop(0, (n - 1) * count, step, 0)
@@ -466,8 +499,10 @@
                     lambda: final_copy(b, end_here, 1).wait_send()
                 )
 
-    if lent:
-        pl.when(at_end)(lambda: lend().wait_send())
+    for k in range(lent):
+        pl.when(at_end)(lambda: lend(k).wait_send())
+        for g in range(1, groups):
+            pl.when(beside)(lambda: spread(k, g).wait_send())
 
 
 def slots_kernel(
@@ -527,9 +562,9 @@
         second_copy(k).wait_send()
 
 
-def reaching(collective_id):
+def reaching(collective_id, grant=48 * 1024 * 1024):
     return pltpu.CompilerParams(
-        collective_id=collective_id, has_side_effects=True, vmem_limit_bytes=48 * 1024 * 1024
+        collective_id=collective_id, has_side_effects=True, vmem_limit_bytes=grant
     )
 
 
@@ -558,7 +593,7 @@
 def mixer(
     ssm_input, decay_log, state_write, state_read, skip_scale, gate_input, ssm_gain, weight, residual_in
 ):
-    n, heads = lax.axis_size("ctx"), lax.axis_size("heads")
+    n, heads, groups = lax.axis_size("ctx"), lax.axis_size("heads"), lax.axis_size("groups")
     rows, columns = ssm_input.shape
     head_count = decay_log.shape[1]
     width = columns // head_count
@@ -574,9 +609,9 @@
     half, strip = out_width // 2, rows // chips
     lane_count = -(-head_count // 128) * 128
     block = (rows, out_width)
-    anywhere = pl.BlockSpec(memory_space=pl.ANY)
+    anywhere = pl.BlockSpec(memory_space=pltpu.HBM)
     return pl.pallas_call(
-        functools.partial(mixer_kernel, n, heads, width, piece, 3, lent),
+        functools.partial(mixer_kernel, n, heads, groups, width, piece, 3, lent),
         out_shape=jax.ShapeDtypeStruct((rows, share * out_width), F32),
         in_specs=[anywhere] * 9,
         out_specs=vmem()[0],
@@ -613,9 +648,9 @@
             dma(9), dma(pairs), dma(pairs),
             dma(n, count), dma(n, count), dma(n, count), dma(n, count),
             dma(2, n), dma(2, n), dma(2, n, chips), dma(2, n, chips), dma(2, n), dma(share, heads),
-            dma(1), dma(1), dma(n),
+            dma(max(lent, 1)), dma(max(lent, 1)), dma(max(lent, 1), groups), dma(max(lent, 1), groups), dma(n),
         ],
-        compiler_params=reaching(1),
+        compiler_params=reaching(1, 67043328),
     )(
         ssm_input, state_write, state_read, decay_log.T, skip_scale.reshape(1, head_count), weight,
         gate_input, ssm_gain.reshape(1, columns), residual_in,

time: 165 us -> 150 us (0.909)
  Pallas kernels: 146 us -> 134 us
  local copies, waits for them, and re-layouts: 8.66 us -> 3.46 us
    pallas_call x1, Pallas kernels: 110 us -> 81.8 us  [mixer(): pl.pallas_call(functools.partial(mixer_kernel, n, heads, groups, width, p...]
    pallas_call x2, Pallas kernels: 35.7 us -> 52.6 us  [through_slots(): pl.pallas_call(functools.partial(slots_kernel, n, heads, width, features)...]
    unnamed x29 -> x19, local copies, waits for them, and re-layouts: 7.44 us -> 0.59 us
    dot_general x1, matrix products: 0.71 us -> 2.72 us  [local(): jnp.dot(scaled, down_latent, preferred_element_type=F32).astype(BF)]
    dot_general x1, matrix products: 3.51 us -> 1.66 us  [local(): jnp.dot(combined.astype(BF), up_latent, preferred_element_type=F32)]
    reshape x2, local copies, waits for them, and re-layouts: 0.21 us -> 1.86 us  [local(): expert_out.astype(BF).reshape(experts_here, n, CAP, heads, piece)]
where the time goes in v3:
time: 150 us; the launch traced here: 149 us
  Pallas kernels  134 us (89%)
  matrix products  8.66 us (6%)
  local copies, waits for them, and re-layouts  3.46 us (2%)
  other arithmetic  2.51 us (2%)
    pallas_call x1, Pallas kernels, mixer(): pl.pallas_call(functools.partial(mixer_kernel, n, heads, groups, width, p...  81.8 us
    pallas_call x2, Pallas kernels, through_slots(): pl.pallas_call(functools.partial(slots_kernel, n, heads, width, features)...  52.6 us
    dot_general x1, matrix products, local(): jnp.einsum('esf,efl->esl', hidden, expert_down, preferred_element_type=F32)  4.02 us

profile of v3, /device:TPU:1, one launch (start us, length us, event | category | flops | bytes accessed | tf_op | source)
XLA Modules:
  0.0 149.3 jit_solution(4121649399484764440)
XLA Ops:
  0.0 0.8 fusion.8
  0.8 0.0 copy-start.7
  0.8 0.6 reduce-window.6
  1.4 0.2 slice_reduce_fusion
  1.6 0.1 add_bitcast_fusion
  1.7 0.1 eq.66
  1.8 0.5 copy-done.3
  2.3 0.7 fusion.11
  3.0 0.0 copy-done.7
  3.0 81.8 %shard_map.154 = f32[256,1024]{1,0:T(8,128)} custom-call(bf16[256,2048]{1,0:T(8,128)(2,1)} %x_hbm.1, bf16[256,128]{1,0:T(8,128)(2,1)} %write_hbm.1, bf16[256,128]{1,0:T(8,128)(2,1)} %read_hbm.1, f32[32,256]{1,0:T(8,128)} %bitcast.56, f32[1,32]{1,0:T(1,128)} %bitcast.58, bf16[2048,1024]{1,0:T(8,128)(2,1)} %weight_hbm.1, bf16[256,2048]{1,0:T(8,128)(2,1)} %gate_hbm.1, ...), custom_call_target="tpu_custom_call" | custom-call | tf_op jit(solution)/shard_map/pallas_call | solution.py:613
  84.9 0.0 copy-start
  84.9 0.0 copy-start.5
  84.9 2.7 %convolution_convert_fusion.1 = bf16[256,1024]{1,0:T(8,128)(2,1)S(1)} fusion(bf16[1024,1024]{1,0:T(8,128)(2,1)} %param.26, f32[256,1024]{1,0:T(8,128)} %shard_map.154, f32[1024]{0:T(1024)} %param.25), kind=kOutput, calls=%fused_computation.2 | convolution fusion | flops 537657344 | bytes 3674112 | tf_op jit(solution)/shard_map/dot_general | solution.py:703
  87.6 0.0 copy-done
  87.6 0.1 multiply_reduce_fusion
  87.8 0.1 broadcast_in_dim.42
  87.9 0.3 convolution_convert_fusion
  88.2 0.1 pad_maximum_fusion.src_ref
  88.3 36.9 %shard_map.155 = bf16[4,4,32,256]{3,2,1,0:T(8,128)(2,1)S(1)} custom-call(bf16[4,4,32,384]{3,2,1,0:T(8,128)(2,1)S(1)} %pad_maximum_fusion.src_ref), custom_call_target="tpu_custom_call" | custom-call | tf_op jit(solution)/shard_map/pallas_call | solution.py:577
  125.2 0.2 copy.30
  125.4 0.2 reshape.105
  125.6 4.0 %convolution_convert_fusion.3 = bf16[2,64,1024]{2,1,0:T(8,128)(2,1)S(1)} fusion(bf16[2,672,1024]{2,1,0:T(8,128)(2,1)} %param.28, bf16[2,64,1024]{2,1,0:T(8,128)(2,1)S(1)} %reshape.105, bf16[2,1024,672]{1,2,0:T(8,128)(2,1)} %param.27), kind=kOutput, calls=%fused_computation.5 | convolution fusion | flops 352710656 | bytes 6029312 | tf_op jit(solution)/shard_map/esf,efl->esl/dot_general | solution.py:725
  129.6 0.0 copy-start.2
  129.6 0.0 copy-start.6
  129.6 0.0 copy-start.4
  129.7 0.0 copy-start.8
  129.7 0.0 copy-start.1
  129.7 0.9 reshape.106
  130.6 1.0 copy.26
  131.6 15.7 %shard_map.156 = bf16[4,4,32,256]{3,2,1,0:T(8,128)(2,1)S(1)} custom-call(bf16[4,4,32,256]{3,2,1,0:T(8,128)(2,1)S(1)} %bitcast.47), custom_call_target="tpu_custom_call" | custom-call | tf_op jit(solution)/shard_map/pallas_call | solution.py:577
  147.3 0.2 copy.27
  147.7 1.7 %fusion = bf16[256,1024]{1,0:T(8,128)(2,1)} fusion(f32[256,1024]{1,0:T(8,128)S(1)} %copy-done, bf16[1024,1024]{1,0:T(8,128)(2,1)S(1)} %copy-done.1, bf16[256,128]{0,1:T(8,128)(2,1)S(1)} %bitcast.55, bf16[128,1024]{1,0:T(8,128)(2,1)S(1)} %bitcast.51), kind=kOutput, calls=%fused_computation.3 | convolution fusion | flops 604766208 | bytes 3997696 | tf_op jit(solution)/shard_map/dot_general | solution.py:731
  (18 shorter events, 0.2 us)
Async XLA Ops:
  0.8 2.2 %copy-start.7 = (pred[256,8]{0,1:T(8,128)(4,1)}, pred[256,8]{0,1:T(8,128)(4,1)S(1)}, u32[]{:S(2)}) copy-start(pred[256,8]{0,1:T(8,128)(4,1)S(1)} %get-tuple-element.11) | copy-start | bytes 6148
  1.7 0.6 copy-start.3
  84.9 2.7 %copy-start = (f32[256,1024]{1,0:T(8,128)S(1)}, f32[256,1024]{1,0:T(8,128)}, u32[]{:S(2)}) copy-start(f32[256,1024]{1,0:T(8,128)} %shard_map.154) | copy-start | bytes 3145732
  84.9 3.0 %copy-start.5 = (pred[256,128]{0,1:T(32,128)(4,1)S(1)}, pred[256,128]{0,1:T(32,128)(4,1)}, u32[]{:S(2)}) copy-start(pred[256,128]{0,1:T(32,128)(4,1)} %fusion.11) | copy-start | bytes 98308
  129.6 17.9 %copy-start.2 = (s32[256,22]{0,1:T(8,128)S(1)}, s32[256,22]{0,1:T(8,128)}, u32[]{:S(2)}) copy-start(s32[256,22]{0,1:T(8,128)} %param.30) | copy-start | bytes 67588
  129.6 17.9 %copy-start.6 = (s32[256,22]{0,1:T(8,128)S(1)}, s32[256,22]{0,1:T(8,128)}, u32[]{:S(2)}) copy-start(s32[256,22]{0,1:T(8,128)} %param.31) | copy-start | bytes 67588
  129.6 17.9 %copy-start.4 = (s32[256,8]{0,1:T(8,128)S(1)}, s32[256,8]{0,1:T(8,128)}, u32[]{:S(2)}) copy-start(s32[256,8]{0,1:T(8,128)} %copy-done.3) | copy-start | bytes 24580
  129.7 17.9 %copy-start.8 = (pred[256,8]{0,1:T(8,128)(4,1)S(1)}, pred[256,8]{0,1:T(8,128)(4,1)}, u32[]{:S(2)}) copy-start(pred[256,8]{0,1:T(8,128)(4,1)} %copy-done.7) | copy-start | bytes 6148
  129.7 18.0 %copy-start.1 = (bf16[1024,1024]{1,0:T(8,128)(2,1)S(1)}, bf16[1024,1024]{1,0:T(8,128)(2,1)}, u32[]{:S(2)}) copy-start(bf16[1024,1024]{1,0:T(8,128)(2,1)} %param.29) | copy-start | bytes 6291460

commit v4 on v3

--- a/solution.py
+++ b/solution.py
@@ -262,9 +262,9 @@
             pl.when(goes_down(p))(lambda: downward(me, p).start())
         return carry
 
-    lax.fori_loop(0, columns // GRP, gate, 0)
     for k in range(lent):
         pl.when(me == 0)(lambda: lend(k).start())
+    lax.fori_loop(0, columns // GRP, gate, 0)
 
     def multiply(slot, b, p):
         step = min(out_width, 256)
@@ -415,45 +415,37 @@
         def at(spot, act):
             pl.when(p == min(spot, count - 1))(lambda: both_sides(s - 1, act))
 
-        at(0, sum_cores)
-        at(1, sum_chips)
+        at(1, sum_cores)
+        at(4, sum_chips)
         def reduce_help(b):
             pl.when(helps(b))(lambda: sum_cores(b, 1))
 
-        for k in range(lent):
-            @pl.when(jnp.logical_and(beside, i == (n - 3) * count + min(2 * (k + 1), count - 1)))
+        if lent:
+            @pl.when(jnp.logical_and(i == 1, beside))
             def _():
-                lend(k).wait_recv()
-                for g in range(1, groups):
-                    spread(k, g).start()
-
-        if lent:
-            @pl.when(i == (n - 2) * count - 1)
-            def _():
-                @pl.when(beside)
-                def _():
-                    for k in range(lent):
-                        for g in range(1, groups):
-                            spread(k, g, True).wait_recv()
-
-                for r in range(n - 2):
-                    both_sides(r, helping)
-
-            @pl.when(i == (n - 2) * count)
-            def _():
-                both_sides(n - 2, helping)
-                for r in range(n - 2):
-                    both_sides(r, reduce_help)
-
-            pl.when(i == (n - 2) * count + 1)(lambda: both_sides(n - 2, reduce_help))
+                for k in range(lent):
+                    for g in range(1, groups):
+                        spread(k, g, True).wait_recv()
+
+            at(2, helping)
+            at(4, reduce_help)
+            pl.when(jnp.logical_and(p == min(7, count - 1), s > 1))(
+                lambda: both_sides(s - 2, combine)
+            )
         return carry
+
+    for k in range(lent):
+        @pl.when(beside)
+        def _():
+            lend(k).wait_recv()
+            for g in range(1, groups):
+                spread(k, g).start()
 
     lax.fori_loop(0, (n - 1) * count, step, 0)
     both_sides(n - 1, sum_cores)
     both_sides(n - 1, sum_chips)
     if lent:
-        for s in range(n - 1):
-            both_sides(s, combine)
+        both_sides(n - 2, combine)
     loads[8].wait()
 
     for j in range(share):

time: 150 us -> 141 us (0.940)
  Pallas kernels: 134 us -> 126 us
    pallas_call x2, Pallas kernels: 52.6 us -> 37.4 us  [through_slots(): pl.pallas_call(functools.partial(slots_kernel, n, heads, width, features)...]
    pallas_call x1, Pallas kernels: 81.8 us -> 88.6 us  [mixer(): pl.pallas_call(functools.partial(mixer_kernel, n, heads, groups, width, p...]
where the time goes in v4:
time: 141 us
  Pallas kernels  126 us (89%)
  matrix products  8.66 us (6%)
  local copies, waits for them, and re-layouts  3.46 us (2%)
  other arithmetic  2.51 us (2%)
    pallas_call x1, Pallas kernels, mixer(): pl.pallas_call(functools.partial(mixer_kernel, n, heads, groups, width, p...  88.6 us
    pallas_call x2, Pallas kernels, through_slots(): pl.pallas_call(functools.partial(slots_kernel, n, heads, width, features)...  37.4 us
    dot_general x1, matrix products, local(): jnp.einsum('esf,efl->esl', hidden, expert_down, preferred_element_type=F32)  4.03 us

profile of v4, /device:TPU:1, one launch (start us, length us, event | category | flops | bytes accessed | tf_op | source)
XLA Modules:
  0.0 141.0 jit_solution(16007711705538641125)
XLA Ops:
  0.0 0.8 fusion.8
  0.8 0.0 copy-start.7
  0.8 0.6 reduce-window.6
  1.4 0.2 slice_reduce_fusion
  1.6 0.1 add_bitcast_fusion
  1.7 0.1 eq.66
  1.8 0.5 copy-done.3
  2.3 0.7 fusion.11
  3.0 0.0 copy-done.7
  3.0 88.6 %shard_map.154 = f32[256,1024]{1,0:T(8,128)} custom-call(bf16[256,2048]{1,0:T(8,128)(2,1)} %x_hbm.1, bf16[256,128]{1,0:T(8,128)(2,1)} %write_hbm.1, bf16[256,128]{1,0:T(8,128)(2,1)} %read_hbm.1, f32[32,256]{1,0:T(8,128)} %bitcast.56, f32[1,32]{1,0:T(1,128)} %bitcast.58, bf16[2048,1024]{1,0:T(8,128)(2,1)} %weight_hbm.1, bf16[256,2048]{1,0:T(8,128)(2,1)} %gate_hbm.1, ...), custom_call_target="tpu_custom_call" | custom-call | tf_op jit(solution)/shard_map/pallas_call | solution.py:605
  91.7 0.0 copy-start
  91.7 0.0 copy-start.5
  91.7 2.7 %convolution_convert_fusion.1 = bf16[256,1024]{1,0:T(8,128)(2,1)S(1)} fusion(bf16[1024,1024]{1,0:T(8,128)(2,1)} %param.26, f32[256,1024]{1,0:T(8,128)} %shard_map.154, f32[1024]{0:T(1024)} %param.25), kind=kOutput, calls=%fused_computation.2 | convolution fusion | flops 537657344 | bytes 3674112 | tf_op jit(solution)/shard_map/dot_general | solution.py:695
  94.4 0.0 copy-done
  94.4 0.1 multiply_reduce_fusion
  94.6 0.1 broadcast_in_dim.42
  94.7 0.3 convolution_convert_fusion
  95.1 0.1 pad_maximum_fusion.src_ref
  95.1 23.5 %shard_map.155 = bf16[4,4,32,256]{3,2,1,0:T(8,128)(2,1)S(1)} custom-call(bf16[4,4,32,384]{3,2,1,0:T(8,128)(2,1)S(1)} %pad_maximum_fusion.src_ref), custom_call_target="tpu_custom_call" | custom-call | tf_op jit(solution)/shard_map/pallas_call | solution.py:569
  118.6 0.2 copy.30
  118.8 0.2 reshape.105
  119.0 4.0 %convolution_convert_fusion.3 = bf16[2,64,1024]{2,1,0:T(8,128)(2,1)S(1)} fusion(bf16[2,672,1024]{2,1,0:T(8,128)(2,1)} %param.28, bf16[2,64,1024]{2,1,0:T(8,128)(2,1)S(1)} %reshape.105, bf16[2,1024,672]{1,2,0:T(8,128)(2,1)} %param.27), kind=kOutput, calls=%fused_computation.5 | convolution fusion | flops 352710656 | bytes 6029312 | tf_op jit(solution)/shard_map/esf,efl->esl/dot_general | solution.py:717
  123.0 0.0 copy-start.2
  123.0 0.0 copy-start.6
  123.1 0.0 copy-start.4
  123.1 0.0 copy-start.8
  123.1 0.0 copy-start.1
  123.1 0.9 reshape.106
  124.0 1.0 copy.26
  125.0 13.9 %shard_map.156 = bf16[4,4,32,256]{3,2,1,0:T(8,128)(2,1)S(1)} custom-call(bf16[4,4,32,256]{3,2,1,0:T(8,128)(2,1)S(1)} %bitcast.47), custom_call_target="tpu_custom_call" | custom-call | tf_op jit(solution)/shard_map/pallas_call | solution.py:569
  138.9 0.2 copy.27
  139.3 1.7 %fusion = bf16[256,1024]{1,0:T(8,128)(2,1)} fusion(f32[256,1024]{1,0:T(8,128)S(1)} %copy-done, bf16[1024,1024]{1,0:T(8,128)(2,1)S(1)} %copy-done.1, bf16[256,128]{0,1:T(8,128)(2,1)S(1)} %bitcast.55, bf16[128,1024]{1,0:T(8,128)(2,1)S(1)} %bitcast.51), kind=kOutput, calls=%fused_computation.3 | convolution fusion | flops 604766208 | bytes 3997696 | tf_op jit(solution)/shard_map/dot_general | solution.py:723
  (18 shorter events, 0.2 us)
Async XLA Ops:
  0.8 2.2 %copy-start.7 = (pred[256,8]{0,1:T(8,128)(4,1)}, pred[256,8]{0,1:T(8,128)(4,1)S(1)}, u32[]{:S(2)}) copy-start(pred[256,8]{0,1:T(8,128)(4,1)S(1)} %get-tuple-element.11) | copy-start | bytes 6148
  1.7 0.6 copy-start.3
  91.7 2.7 %copy-start = (f32[256,1024]{1,0:T(8,128)S(1)}, f32[256,1024]{1,0:T(8,128)}, u32[]{:S(2)}) copy-start(f32[256,1024]{1,0:T(8,128)} %shard_map.154) | copy-start | bytes 3145732
  91.7 3.0 %copy-start.5 = (pred[256,128]{0,1:T(32,128)(4,1)S(1)}, pred[256,128]{0,1:T(32,128)(4,1)}, u32[]{:S(2)}) copy-start(pred[256,128]{0,1:T(32,128)(4,1)} %fusion.11) | copy-start | bytes 98308
  123.0 16.1 %copy-start.2 = (s32[256,22]{0,1:T(8,128)S(1)}, s32[256,22]{0,1:T(8,128)}, u32[]{:S(2)}) copy-start(s32[256,22]{0,1:T(8,128)} %param.30) | copy-start | bytes 67588
  123.0 16.1 %copy-start.6 = (s32[256,22]{0,1:T(8,128)S(1)}, s32[256,22]{0,1:T(8,128)}, u32[]{:S(2)}) copy-start(s32[256,22]{0,1:T(8,128)} %param.31) | copy-start | bytes 67588
  123.1 16.2 %copy-start.4 = (s32[256,8]{0,1:T(8,128)S(1)}, s32[256,8]{0,1:T(8,128)}, u32[]{:S(2)}) copy-start(s32[256,8]{0,1:T(8,128)} %copy-done.3) | copy-start | bytes 24580
  123.1 16.2 %copy-start.8 = (pred[256,8]{0,1:T(8,128)(4,1)S(1)}, pred[256,8]{0,1:T(8,128)(4,1)}, u32[]{:S(2)}) copy-start(pred[256,8]{0,1:T(8,128)(4,1)} %copy-done.7) | copy-start | bytes 6148
  123.1 16.2 %copy-start.1 = (bf16[1024,1024]{1,0:T(8,128)(2,1)S(1)}, bf16[1024,1024]{1,0:T(8,128)(2,1)}, u32[]{:S(2)}) copy-start(bf16[1024,1024]{1,0:T(8,128)(2,1)} %param.29) | copy-start | bytes 6291460

commit v5 on v4

--- a/solution.py
+++ b/solution.py
@@ -7,9 +7,7 @@
 from jax.experimental.pallas import tpu as pltpu
 from jax.sharding import PartitionSpec as P
 
-D = 4096
 GRP = 1024
-LAT = 1024
 CAP = 16
 LENT_NUM, LENT_DEN = 3, 8
 
@@ -36,10 +34,6 @@
     pl.semaphore_wait(pltpu.get_barrier_semaphore(), count)
 
 
-def one_if(condition):
-    return jnp.where(condition, 1, 0)
-
-
 def remote(src, dst, send, recv, device):
     return pltpu.make_async_remote_copy(
         src_ref=src, dst_ref=dst, send_sem=send, recv_sem=recv, device_id=device, device_id_type=MESH
@@ -51,16 +45,22 @@
     return jnp.where(lane < width, first, second)
 
 
-def mixer_kernel(
+def layer_kernel(
     n, heads, groups, width, piece, lag, lent,
     x_hbm, write_hbm, read_hbm, decay_hbm, skip_hbm, weight_hbm, gate_hbm, gain_hbm, resid_hbm,
+    ids_hbm, fixed_hbm, moe_hbm, latent_hbm, grow_hbm, shrink_hbm, lift_hbm,
     out_ref,
     x_ref, write_ref, read_ref, decay_ref, skip_ref, weight_ref, gate_ref, gain_ref, resid_ref,
+    ids_ref, fixed_ref, moe_ref, latent_ref, grow_ref, shrink_ref, lift_ref,
     cum, cum_rows, skips, inter,
     mixed, state, ends, prior, outgoing, gated,
     blocks, acc, parts, core_in, chip_out, x_in, fin_out, final, borrowed, strips,
+    residual, chosen, weights, placed, table, square_out, square_in,
+    slots_out, slots_in, middle, gathered, back_out, back_in, back_middle, returned,
     load_sem, chain_send, chain_recv, up_send, up_recv, down_send, down_recv,
     core_send, core_recv, x_send, x_recv, fin_send, fin_recv, lend_send, lend_recv, spread_send, spread_recv, strip_recv,
+    square_send, square_recv, first_send, first_recv, second_send, second_recv,
+    third_send, third_recv, fourth_send, fourth_recv, fifth_send, fifth_recv, sixth_send, sixth_recv,
 ):
     me, head, group = lax.axis_index("ctx"), lax.axis_index("heads"), lax.axis_index("groups")
     rows, columns = x_ref.shape
@@ -89,10 +89,13 @@
                 (x_hbm, x_ref), (write_hbm, write_ref), (read_hbm, read_ref), (decay_hbm, decay_ref),
                 (skip_hbm, skip_ref), (weight_hbm, weight_ref), (gate_hbm, gate_ref),
                 (gain_hbm, gain_ref), (resid_hbm, resid_ref),
+                (ids_hbm, ids_ref), (fixed_hbm, fixed_ref), (moe_hbm, moe_ref),
+                (latent_hbm, latent_ref), (grow_hbm, grow_ref), (shrink_hbm, shrink_ref),
+                (lift_hbm, lift_ref),
             ]
         )
     ]
-    for load in loads:
+    for load in loads[:8]:
         load.start()
     for i in range(n):
         for j in range(heads):
@@ -123,6 +126,8 @@
     inter[...] = jnp.where(t >= s, product, 0.0)
     greeted(n * heads + groups - 2)
 
+    for load in loads[8:]:
+        load.start()
     share_rows = piece // groups
 
     def lend(k):
@@ -381,6 +386,23 @@
     lax.fori_loop(0, count, own, 0)
     round_partial(me, 0)
 
+    loads[9].wait()
+    loads[10].wait()
+    wave = chosen.shape[0]
+    for e in range(wave):
+        named = ids_ref[...] == e
+        chosen[e : e + 1, :] = jnp.sum(jnp.where(named, 1.0, 0.0), axis=0, keepdims=True)
+        weights[e : e + 1, :] = jnp.sum(jnp.where(named, fixed_ref[...], 0), axis=0, keepdims=True)
+    upto = jnp.where(t <= s, 1.0, 0.0).astype(BF)
+    taken = jnp.dot(chosen[...].astype(BF), upto, preferred_element_type=F32)
+    slot = lax.broadcasted_iota(jnp.int32, (CAP, rows), 0).astype(F32) + 1.0
+    for e in range(wave):
+        here = jnp.logical_and(chosen[e : e + 1, :] > 0.5, taken[e : e + 1, :] == slot)
+        weight = weights[e : e + 1, :].astype(F32) / 65536.0
+        part = slice(e * CAP, (e + 1) * CAP)
+        placed[part] = jnp.where(here, 1.0, 0.0).astype(BF)
+        table[part] = jnp.where(here, weight, 0.0).astype(BF)
+
     def around(s, act):
         low, high = me - s, me + s
         pl.when(low >= 0)(lambda: act(jnp.maximum(low, 0), 0))
@@ -465,10 +487,169 @@
 
             part = slice((k // cores) * strip, (k // cores + 1) * strip)
             lo = j * out_width + (k % cores) * half
-            out_ref[part, lo : lo + half] = (
+            residual[part, lo : lo + half] = (
                 resid_ref[part, lo : lo + half].astype(F32) + final[j, k].astype(F32)
             )
 
+    for load in loads[11:]:
+        load.wait()
+    latent_width = latent_ref.shape[1]
+    strand = latent_width // heads
+    features = residual.shape[1] * heads
+    experts_here = grow_ref.shape[0]
+    slot_rows = experts_here * CAP
+    held = residual[...]
+    scaled = (held * moe_ref[...]).astype(BF)
+    picked = jnp.dot(placed[...], scaled, preferred_element_type=F32).astype(BF)
+    power = jnp.sum(held * held, axis=1, keepdims=True)
+    power = jnp.transpose(jnp.broadcast_to(power, (rows, 128)))[:8, :]
+    square_out[...] = lax.dot_general(
+        power, placed[...].astype(F32), (((1,), (1,)), ((), ())),
+        precision=lax.Precision.HIGHEST, preferred_element_type=F32,
+    )
+
+    def square_copy(k):
+        return remote(
+            square_out, square_in.at[k], square_send.at[k], square_recv.at[k],
+            {"heads": (head + k) % heads},
+        )
+
+    def first_copy(k):
+        to = (head + k) % heads
+        return remote(
+            slots_out.at[k], slots_in.at[k], first_send.at[k], first_recv.at[k], {"heads": to}
+        )
+
+    for k in range(1, heads):
+        square_copy(k).start()
+    for k in [*range(1, heads), 0]:
+        to = (head + k) % heads
+        lane = pl.ds(pl.multiple_of(to * strand, strand), strand)
+        value = jnp.dot(picked, latent_ref[:, lane], preferred_element_type=F32).astype(BF)
+        for z in range(n):
+            slots_out[k, z] = value[z * slot_rows : (z + 1) * slot_rows]
+        if k:
+            first_copy(k).start()
+
+    def second_copy(k):
+        to = (me + k) % n
+        return remote(
+            middle.at[to], gathered.at[head, me], second_send.at[k], second_recv.at[k], {"ctx": to}
+        )
+
+    def third_copy(k, j):
+        spot = gathered.at[head, (me + n - k) % n]
+        return remote(
+            spot, spot, third_send.at[k, j], third_recv.at[k, j], {"heads": (head + j) % heads}
+        )
+
+    power = square_out[...]
+    for k in range(1, heads):
+        square_copy(k).wait_recv()
+        power = power + square_in[k]
+    scale = lax.rsqrt(power / features + epsilon)
+    scale = jnp.transpose(jnp.broadcast_to(scale[0:1, :], (128, scale.shape[1])))
+    for k in range(1, heads):
+        first_copy(k).wait_recv()
+    for z in range(n):
+        total = slots_out[0, z].astype(F32)
+        for k in range(1, heads):
+            total = total + slots_in[k, z].astype(F32)
+        middle[z] = (total * scale[z * slot_rows : (z + 1) * slot_rows, 0:1]).astype(BF)
+    for k in range(1, n):
+        second_copy(k).start()
+    gathered[head, me] = middle[me]
+    for k in range(n):
+        if k:
+            second_copy(k).wait_recv()
+        for j in range(1, heads):
+            third_copy(k, j).start()
+    for k in range(n):
+        for j in range(1, heads):
+            third_copy(k, j).wait_recv()
+
+    def fourth_copy(e, k):
+        return remote(
+            back_out.at[e, (head + k) % heads], back_in.at[e, k], fourth_send.at[e, k],
+            fourth_recv.at[e, k], {"heads": (head + k) % heads},
+        )
+
+    def fifth_copy(e, k):
+        to = (me + k) % n
+        return remote(
+            back_middle.at[e, to], returned.at[head, me, e], fifth_send.at[e, k],
+            fifth_recv.at[e, k], {"ctx": to},
+        )
+
+    def sixth_copy(k, j):
+        spot = returned.at[head, (me + n - k) % n]
+        return remote(
+            spot, spot, sixth_send.at[k, j], sixth_recv.at[k, j], {"heads": (head + j) % heads}
+        )
+
+    for e in range(experts_here):
+        part = slice(e * CAP, (e + 1) * CAP)
+        fed = jnp.concatenate(
+            [gathered[h, :, part].reshape(n * CAP, strand) for h in range(heads)], axis=1
+        )
+        hidden = lax.dot_general(
+            fed, grow_ref[e], (((1,), (1,)), ((), ())), preferred_element_type=F32
+        )
+        hidden = (jnp.maximum(hidden, 0.0) ** 2).astype(BF)
+        value = jnp.dot(hidden, shrink_ref[e], preferred_element_type=F32).astype(BF)
+        for h in range(heads):
+            for z in range(n):
+                back_out[e, h, z] = value[z * CAP : (z + 1) * CAP, h * strand : (h + 1) * strand]
+        for k in range(1, heads):
+            fourth_copy(e, k).start()
+    for e in range(experts_here):
+        for k in range(1, heads):
+            fourth_copy(e, k).wait_recv()
+        total = back_out[e, head].astype(F32)
+        for k in range(1, heads):
+            total = total + back_in[e, k].astype(F32)
+        back_middle[e] = total.astype(BF)
+        for k in range(1, n):
+            fifth_copy(e, k).start()
+        returned[head, me, e] = back_middle[e, me]
+    for k in range(n):
+        if k:
+            for e in range(experts_here):
+                fifth_copy(e, k).wait_recv()
+        for j in range(1, heads):
+            sixth_copy(k, j).start()
+    for k in range(n):
+        for j in range(1, heads):
+            sixth_copy(k, j).wait_recv()
+    combined = jnp.concatenate(
+        [
+            lax.dot_general(
+                table[...], returned[h].reshape(wave * CAP, strand), (((0,), (0,)), ((), ())),
+                preferred_element_type=F32,
+            ).astype(BF)
+            for h in range(heads)
+        ],
+        axis=1,
+    )
+    lift_step = min(256, residual.shape[1])
+    for lo in range(0, residual.shape[1], lift_step):
+        part = slice(lo, lo + lift_step)
+        value = jnp.dot(combined, lift_ref[:, part], preferred_element_type=F32)
+        out_ref[:, part] = (residual[:, part] + value).astype(BF)
+
+    for k in range(1, heads):
+        square_copy(k).wait_send()
+        first_copy(k).wait_send()
+        for e in range(experts_here):
+            fourth_copy(e, k).wait_send()
+    for k in range(n):
+        for j in range(1, heads):
+            third_copy(k, j).wait_send()
+            sixth_copy(k, j).wait_send()
+        if k:
+            second_copy(k).wait_send()
+            for e in range(experts_here):
+                fifth_copy(e, k).wait_send()
     for q in range(pairs):
         pl.when(has_next)(lambda: chain_copy(q).wait_send())
     for b in range(n):
@@ -497,63 +678,6 @@
             pl.when(beside)(lambda: spread(k, g).wait_send())
 
 
-def slots_kernel(
-    n, heads, width, features, src_ref, out_ref,
-    first, middle, second, third,
-    first_send, first_recv, second_send, second_recv, third_send, third_recv,
-):
-    me, head = lax.axis_index("ctx"), lax.axis_index("heads")
-
-    for k in range(1, heads):
-        greet({"heads": (head + k) % heads})
-    for k in range(1, n):
-        greet({"ctx": (me + k) % n})
-    greeted(heads + n - 2)
-
-    def first_copy(k):
-        to = (head + k) % heads
-        return remote(
-            src_ref.at[to], first.at[k], first_send.at[k], first_recv.at[k], {"heads": to}
-        )
-
-    def second_copy(k):
-        to = (me + k) % n
-        return remote(
-            middle.at[to], second.at[me], second_send.at[k], second_recv.at[k], {"ctx": to}
-        )
-
-    def third_copy(k):
-        to = (head + k) % heads
-        return remote(second, third.at[k], third_send.at[k], third_recv.at[k], {"heads": to})
-
-    for k in range(1, heads):
-        first_copy(k).start()
-    total = src_ref[head].astype(F32)
-    for k in range(1, heads):
-        first_copy(k).wait_recv()
-        total = total + first[k].astype(F32)
-    if src_ref.shape[-1] > width:
-        power = total[:, :, width : width + 1]
-        total = total[:, :, :width] * lax.rsqrt(power / features + epsilon)
-    middle[...] = total.astype(BF)
-    for k in range(1, n):
-        second_copy(k).start()
-    second[me] = middle[me]
-    for k in range(1, n):
-        second_copy(k).wait_recv()
-    for k in range(1, heads):
-        third_copy(k).start()
-    out_ref[head] = second[...]
-    for k in range(1, heads):
-        third_copy(k).wait_recv()
-        out_ref[(head + heads - k) % heads] = third[k]
-    for k in range(1, heads):
-        first_copy(k).wait_send()
-        third_copy(k).wait_send()
-    for k in range(1, n):
-        second_copy(k).wait_send()
-
-
 def reaching(collective_id, grant=48 * 1024 * 1024):
     return pltpu.CompilerParams(
         collective_id=collective_id, has_side_effects=True, vmem_limit_bytes=grant
@@ -564,26 +688,23 @@
     return pltpu.SemaphoreType.DMA(shape)
 
 
-def through_slots(pieces, width, features, collective_id):
-    heads, n, rows, wide = pieces.shape
-    return pl.pallas_call(
-        functools.partial(slots_kernel, n, heads, width, features),
-        out_shape=jax.ShapeDtypeStruct((heads, n, rows, width), BF),
-        in_specs=vmem(),
-        out_specs=vmem()[0],
-        scratch_shapes=[
-            pltpu.VMEM((heads, n, rows, wide), BF),
-            pltpu.VMEM((n, rows, width), BF),
-            pltpu.VMEM((n, rows, width), BF),
-            pltpu.VMEM((heads, n, rows, width), BF),
-            dma(heads), dma(heads), dma(n), dma(n), dma(heads), dma(heads),
-        ],
-        compiler_params=reaching(collective_id),
-    )(pieces)
-
-
-def mixer(
-    ssm_input, decay_log, state_write, state_read, skip_scale, gate_input, ssm_gain, weight, residual_in
+def local(
+    ssm_input,
+    decay_log,
+    state_write,
+    state_read,
+    skip_scale,
+    gate_input,
+    ssm_gain,
+    weight,
+    residual_in,
+    moe_gain,
+    down_latent,
+    expert_up,
+    expert_down,
+    up_latent,
+    expert_ids,
+    combine_fixed,
 ):
     n, heads, groups = lax.axis_size("ctx"), lax.axis_size("heads"), lax.axis_size("groups")
     rows, columns = ssm_input.shape
@@ -601,11 +722,18 @@
     half, strip = out_width // 2, rows // chips
     lane_count = -(-head_count // 128) * 128
     block = (rows, out_width)
+    features = residual_in.shape[1]
+    experts_here = expert_up.shape[0]
+    wave = experts_here * n
+    slot_rows = experts_here * CAP
+    strand = down_latent.shape[1] // heads
+    grow = expert_up.transpose(0, 2, 1)
+    ids, fixed = expert_ids.T, combine_fixed.T
     anywhere = pl.BlockSpec(memory_space=pltpu.HBM)
     return pl.pallas_call(
-        functools.partial(mixer_kernel, n, heads, groups, width, piece, 3, lent),
-        out_shape=jax.ShapeDtypeStruct((rows, share * out_width), F32),
-        in_specs=[anywhere] * 9,
+        functools.partial(layer_kernel, n, heads, groups, width, piece, 3, lent),
+        out_shape=jax.ShapeDtypeStruct((rows, features), BF),
+        in_specs=[anywhere] * 16,
         out_specs=vmem()[0],
         scratch_shapes=[
             pltpu.VMEM((rows, columns), BF),
@@ -617,6 +745,13 @@
             pltpu.VMEM((rows, columns), BF),
             pltpu.VMEM((1, columns), F32),
             pltpu.VMEM(residual_in.shape, BF),
+            pltpu.VMEM(ids.shape, jnp.int32),
+            pltpu.VMEM(fixed.shape, jnp.int32),
+            pltpu.VMEM((1, features), F32),
+            pltpu.VMEM(down_latent.shape, BF),
+            pltpu.VMEM(grow.shape, BF),
+            pltpu.VMEM(expert_down.shape, BF),
+            pltpu.VMEM(up_latent.shape, BF),
             pltpu.VMEM((rows, lane_count), F32),
             pltpu.VMEM((head_count, rows), F32),
             pltpu.VMEM((8, lane_count), F32),
@@ -637,91 +772,35 @@
             pltpu.VMEM((share, heads, strip, half), BF),
             pltpu.VMEM((max(lent, 1) * piece, out_width), BF),
             pltpu.VMEM((n, strip, half), BF),
-            dma(9), dma(pairs), dma(pairs),
+            pltpu.VMEM((rows, features), F32),
+            pltpu.VMEM((wave, rows), F32),
+            pltpu.VMEM((wave, rows), jnp.int32),
+            pltpu.VMEM((wave * CAP, rows), BF),
+            pltpu.VMEM((wave * CAP, rows), BF),
+            pltpu.VMEM((8, wave * CAP), F32),
+            pltpu.VMEM((heads, 8, wave * CAP), F32),
+            pltpu.VMEM((heads, n, slot_rows, strand), BF),
+            pltpu.VMEM((heads, n, slot_rows, strand), BF),
+            pltpu.VMEM((n, slot_rows, strand), BF),
+            pltpu.VMEM((heads, n, slot_rows, strand), BF),
+            pltpu.VMEM((experts_here, heads, n, CAP, strand), BF),
+            pltpu.VMEM((experts_here, heads, n, CAP, strand), BF),
+            pltpu.VMEM((experts_here, n, CAP, strand), BF),
+            pltpu.VMEM((heads, n, experts_here, CAP, strand), BF),
+            dma(16), dma(pairs), dma(pairs),
             dma(n, count), dma(n, count), dma(n, count), dma(n, count),
             dma(2, n), dma(2, n), dma(2, n, chips), dma(2, n, chips), dma(2, n), dma(share, heads),
             dma(max(lent, 1)), dma(max(lent, 1)), dma(max(lent, 1), groups), dma(max(lent, 1), groups), dma(n),
+            dma(heads), dma(heads), dma(heads), dma(heads), dma(n), dma(n),
+            dma(n, heads), dma(n, heads), dma(experts_here, heads), dma(experts_here, heads),
+            dma(experts_here, n), dma(experts_here, n), dma(n, heads), dma(n, heads),
         ],
         compiler_params=reaching(1, 67043328),
     )(
         ssm_input, state_write, state_read, decay_log.T, skip_scale.reshape(1, head_count), weight,
         gate_input, ssm_gain.reshape(1, columns), residual_in,
-    )
-
-
-def local(
-    ssm_input,
-    decay_log,
-    state_write,
-    state_read,
-    skip_scale,
-    gate_input,
-    ssm_gain,
-    out_weight,
-    residual_in,
-    moe_gain,
-    down_latent,
-    expert_up,
-    expert_down,
-    up_latent,
-    expert_ids,
-    combine_fixed,
-):
-    row_count = ssm_input.shape[0]
-    n, heads = lax.axis_size("ctx"), lax.axis_size("heads")
-    features = residual_in.shape[1] * heads
-    latent_width = down_latent.shape[1]
-    piece = latent_width // heads
-    experts_here = expert_up.shape[0]
-    wave_size = experts_here * n
-    slot_rows = experts_here * CAP
-
-    matches = expert_ids[:, :, None] == jnp.arange(wave_size)[None, None, :]
-    chosen = jnp.any(matches, axis=1).astype(jnp.int32)
-    weight_fixed = jnp.sum(jnp.where(matches, combine_fixed[:, :, None], 0), axis=1)
-    slot_index = jnp.cumsum(chosen, axis=0) - 1
-    placed = (chosen[:, :, None] == 1) & (slot_index[:, :, None] == jnp.arange(CAP)[None, None, :])
-    route_weight = (weight_fixed.astype(F32) / 65536.0).astype(BF)
-    combine_table = jnp.where(placed, route_weight[:, :, None], jnp.zeros((), BF)).reshape(
-        row_count, wave_size * CAP
-    )
-    placed = placed.astype(BF).reshape(row_count, wave_size * CAP)
-
-    residual = mixer(
-        ssm_input, decay_log, state_write, state_read, skip_scale, gate_input, ssm_gain,
-        out_weight, residual_in,
-    )
-    scaled = (residual * moe_gain).astype(BF)
-    latent_part = jnp.dot(scaled, down_latent, preferred_element_type=F32).astype(BF)
-    squares = jnp.sum(residual * residual, axis=1).astype(BF)
-    side = jnp.concatenate(
-        [latent_part, jnp.broadcast_to(squares[:, None], (row_count, 128))], axis=1
-    )
-    slots = lax.dot_general(
-        placed, side, (((0,), (0,)), ((), ())), preferred_element_type=F32
-    ).astype(BF)
-    slots = slots.reshape(n, slot_rows, latent_width + 128)
-    pieces = jnp.stack(
-        [
-            jnp.concatenate(
-                [slots[:, :, h * piece : (h + 1) * piece], slots[:, :, latent_width:]], axis=2
-            )
-            for h in range(heads)
-        ]
-    )
-    incoming = through_slots(pieces, piece, features, 3)
-    incoming = incoming.reshape(heads, n, experts_here, CAP, piece).transpose(2, 1, 3, 0, 4)
-    incoming = incoming.reshape(experts_here, n * CAP, latent_width)
-    hidden = jnp.einsum("esl,elf->esf", incoming, expert_up, preferred_element_type=F32)
-    hidden = (jnp.maximum(hidden, 0.0) ** 2).astype(BF)
-    expert_out = jnp.einsum("esf,efl->esl", hidden, expert_down, preferred_element_type=F32)
-    expert_out = expert_out.astype(BF).reshape(experts_here, n, CAP, heads, piece)
-    expert_out = expert_out.transpose(3, 1, 0, 2, 4).reshape(heads, n, slot_rows, piece)
-    returned = through_slots(expert_out, piece, features, 4)
-    returned = returned.transpose(1, 2, 0, 3).reshape(wave_size * CAP, latent_width)
-    combined = jnp.dot(combine_table, returned, preferred_element_type=F32)
-    moe_out = jnp.dot(combined.astype(BF), up_latent, preferred_element_type=F32)
-    return (residual + moe_out).astype(BF)
+        ids, fixed, moe_gain.reshape(1, features), down_latent, grow, expert_down, up_latent,
+    )
 
 
 def solution(mesh):

time: 141 us -> 127 us (0.901)
  matrix products: 8.66 us -> 0 us
  other arithmetic: 2.51 us -> 0 us
  Pallas kernels: 126 us -> 124 us
  local copies, waits for them, and re-layouts: 3.46 us -> 1.87 us
    dot_general x4 -> x0, matrix products: 8.66 us -> none  [the longest x1 4.03 us: local(): jnp.einsum('esf,efl->esl', hidden, expert_down, preferred_element_type=F32)]
    reshape x4 -> x0, local copies, waits for them, and re-layouts: 2.24 us -> none  [the longest x2 1.86 us: local(): expert_out.astype(BF).reshape(experts_here, n, CAP, heads, piece)]
    pallas_call x3 -> x1, Pallas kernels: 126 us -> 124 us  [local(): pl.pallas_call(functools.partial(layer_kernel, n, heads, groups, width, p...]
where the time goes in v5:
time: 127 us; the launch traced here: 126 us
  Pallas kernels  124 us (98%)
  local copies, waits for them, and re-layouts  1.87 us (1%)
    pallas_call x1, Pallas kernels, local(): pl.pallas_call(functools.partial(layer_kernel, n, heads, groups, width, p...  124 us

profile of v5, /device:TPU:1, one launch (start us, length us, event | category | flops | bytes accessed | tf_op | source)
XLA Modules:
  0.0 126.0 jit_solution(16693166656013063816)
XLA Ops:
  0.0 124.1 %shard_map.154 = bf16[256,1024]{1,0:T(8,128)(2,1)} custom-call(bf16[256,2048]{1,0:T(8,128)(2,1)} %x_hbm.1, bf16[256,128]{1,0:T(8,128)(2,1)} %write_hbm.1, bf16[256,128]{1,0:T(8,128)(2,1)} %read_hbm.1, f32[32,256]{1,0:T(8,128)} %bitcast.8, f32[1,32]{1,0:T(1,128)} %bitcast.13, bf16[2048,1024]{1,0:T(8,128)(2,1)} %weight_hbm.1, bf16[256,2048]{1,0:T(8,128)(2,1)} %gate_hbm.1, ...), custom_call_target="tpu_custom_call" | custom-call | tf_op jit(solution)/shard_map/pallas_call | solution.py:733
  124.2 1.9 %copy.18 = bf16[256,1024]{1,0:T(8,128)(2,1)} copy(bf16[256,1024]{1,0:T(8,128)(2,1)} %shard_map.154) | data formatting | bytes 1048576

commit v6 on v5

--- a/solution.py
+++ b/solution.py
@@ -9,7 +9,8 @@
 
 GRP = 1024
 CAP = 16
-LENT_NUM, LENT_DEN = 3, 8
+LENT_NUM, LENT_DEN = 1, 2
+WAVES = 4
 
 
 epsilon = 1e-05
@@ -46,7 +47,7 @@
 
 
 def layer_kernel(
-    n, heads, groups, width, piece, lag, lent,
+    n, heads, groups, width, piece, lag, lent, waves,
     x_hbm, write_hbm, read_hbm, decay_hbm, skip_hbm, weight_hbm, gate_hbm, gain_hbm, resid_hbm,
     ids_hbm, fixed_hbm, moe_hbm, latent_hbm, grow_hbm, shrink_hbm, lift_hbm,
     out_ref,
@@ -54,10 +55,11 @@
     ids_ref, fixed_ref, moe_ref, latent_ref, grow_ref, shrink_ref, lift_ref,
     cum, cum_rows, skips, inter,
     mixed, state, ends, prior, outgoing, gated,
-    blocks, acc, parts, core_in, chip_out, x_in, fin_out, final, borrowed, strips,
+    kept, rest, acc, parts, core_in, chip_out, x_in, fin_out, final, borrowed, strips,
     residual, chosen, weights, placed, table, square_out, square_in,
     slots_out, slots_in, middle, gathered, back_out, back_in, back_middle, returned,
     load_sem, chain_send, chain_recv, up_send, up_recv, down_send, down_recv,
+    up_rest_send, up_rest_recv, down_rest_send, down_rest_recv,
     core_send, core_recv, x_send, x_recv, fin_send, fin_recv, lend_send, lend_recv, spread_send, spread_recv, strip_recv,
     square_send, square_recv, first_send, first_recv, second_send, second_recv,
     third_send, third_recv, fourth_send, fourth_recv, fifth_send, fifth_recv, sixth_send, sixth_recv,
@@ -73,10 +75,12 @@
     cores = 2
     chips = heads // cores
     core, chip = head % cores, head // cores
-    half, strip = out_width // cores, rows // chips
+    half, band_rows = out_width // cores, rows // waves
+    strip = band_rows // chips
     has_prev, has_next = me > 0, me < n - 1
     prev, after = jnp.maximum(me - 1, 0), jnp.minimum(me + 1, n - 1)
     keep = count - lent
+    keep_width = keep * piece
     at_end = jnp.logical_or(me == 0, me == n - 1)
     beside = jnp.logical_or(me == 1, me == n - 2)
     end_here = jnp.where(me == 1, 0, n - 1)
@@ -211,40 +215,31 @@
 
         pl.when(has_next)(lambda: chain_copy(q).start())
 
-    def advance(i, carry):
-        pl.when(i < pairs)(lambda: scan(i))
-        q = i - lag * me
-        pl.when(jnp.logical_and(q >= 0, q < pairs))(lambda: chain(q))
-        return carry
-
-    lax.fori_loop(0, pairs + lag * (n - 1), advance, 0)
-
-    def upward(b, p):
-        spot = blocks.at[b, p]
-        return remote(spot, spot, up_send.at[b, p], up_recv.at[b, p], {"ctx": after})
-
-    def downward(b, p):
-        spot = blocks.at[b, p]
-        return remote(spot, spot, down_send.at[b, p], down_recv.at[b, p], {"ctx": prev})
-
-    pl.when(me < n - 1)(lambda: loads[5].wait())
-
-    def goes_up(p):
-        return jnp.logical_and(has_next, jnp.logical_or(p < keep, me + 1 < n - 1))
-
-    def goes_down(p):
-        return jnp.logical_and(has_prev, jnp.logical_or(p < keep, me > 1))
-
-    def needed(p):
-        return jnp.logical_or(p < keep, jnp.logical_not(at_end))
+    def across(ref, sems, b, r, to):
+        spot = ref.at[b, r]
+        return remote(spot, spot, sems[0].at[b, r], sems[1].at[b, r], {"ctx": to})
+
+    def upward(b, r):
+        return across(kept, (up_send, up_recv), b, r, after)
+
+    def downward(b, r):
+        return across(kept, (down_send, down_recv), b, r, prev)
+
+    def upward_rest(b, r):
+        return across(rest, (up_rest_send, up_rest_recv), b, r, after)
+
+    def downward_rest(b, r):
+        return across(rest, (down_rest_send, down_rest_recv), b, r, prev)
+
+    rest_up = jnp.logical_and(has_next, me + 1 < n - 1)
+    rest_down = jnp.logical_and(has_prev, me > 1)
+    inner = jnp.logical_not(at_end)
 
     group_pairs = GRP // span
-    group_pieces = GRP // piece
-    piece_pairs = piece // span
     loads[6].wait()
     loads[7].wait()
 
-    def gate(g, carry):
+    def gate(g):
         squares = jnp.zeros((rows, span), F32)
         for i in range(group_pairs):
             p = g * group_pairs + i
@@ -259,67 +254,97 @@
         for i in range(group_pairs):
             p = g * group_pairs + i
             value = (gated[i] * scale * gain_ref[:, lanes(p)]).astype(BF)
-            lo = (i % piece_pairs) * span
-            blocks[me, g * group_pieces + i // piece_pairs, :, lo : lo + span] = value
-        for k in range(group_pieces):
-            p = g * group_pieces + k
-            pl.when(goes_up(p))(lambda: upward(me, p).start())
-            pl.when(goes_down(p))(lambda: downward(me, p).start())
+            ref, lo = (kept, p * span) if p * span < keep_width else (rest, p * span - keep_width)
+            for r in range(waves):
+                ref[me, r, :, lo : lo + span] = value[r * band_rows : (r + 1) * band_rows]
+
+    early = keep_width // GRP if lent and keep_width % GRP == 0 else 0
+
+    def begin_down():
+        for r in range(waves):
+            pl.when(has_prev)(lambda: downward(me, r).start())
+
+    def advance(i, carry):
+        pl.when(i < pairs)(lambda: scan(i))
+        q = i - lag * me
+        pl.when(jnp.logical_and(q >= 0, q < pairs))(lambda: chain(q))
+        if early:
+            @pl.when(i == jnp.maximum(pairs - 1, early * group_pairs - 1 + lag * me))
+            def _():
+                for g in range(early):
+                    gate(g)
+                begin_down()
+
         return carry
 
+    lax.fori_loop(0, pairs + lag * (n - 1), advance, 0)
+    pl.when(me < n - 1)(lambda: loads[5].wait())
     for k in range(lent):
         pl.when(me == 0)(lambda: lend(k).start())
-    lax.fori_loop(0, columns // GRP, gate, 0)
-
-    def multiply(slot, b, p):
-        step = min(out_width, 256)
-        fed = blocks[b, p]
-        for lo in range(0, out_width, step):
-            held = acc[slot, :, lo : lo + step]
-            part = weight_ref[pl.ds(pl.multiple_of(p * piece, piece), piece), lo : lo + step]
-            acc[slot, :, lo : lo + step] = jnp.where(p == 0, 0.0, held) + jnp.dot(
-                fed, part, preferred_element_type=F32
+    for g in range(early, columns // GRP):
+        gate(g)
+    if not early:
+        begin_down()
+    for r in range(waves):
+        pl.when(has_next)(lambda: upward(me, r).start())
+    if lent:
+        for r in range(waves):
+            pl.when(rest_up)(lambda: upward_rest(me, r).start())
+            pl.when(rest_down)(lambda: downward_rest(me, r).start())
+
+    col_step = min(out_width, 256)
+
+    def multiply(slot, b, r):
+        for lo in range(0, out_width, col_step):
+            acc[slot, r, :, lo : lo + col_step] = jnp.dot(
+                kept[b, r], weight_ref[:keep_width, lo : lo + col_step], preferred_element_type=F32
             )
 
-    def core_copy(b, kind):
-        return remote(
-            parts.at[kind, b, 1 - core], core_in.at[kind, b], core_send.at[kind, b],
-            core_recv.at[kind, b], {"heads": head + 1 - 2 * core},
-        )
-
-    def round_partial(b, slot, kind=0):
+    def multiply_rest(slot, b, r):
+        for lo in range(0, out_width, col_step):
+            acc[slot, r, :, lo : lo + col_step] += jnp.dot(
+                rest[b, r], weight_ref[keep_width:, lo : lo + col_step], preferred_element_type=F32
+            )
+
+    def core_copy(b, r, kind):
+        return remote(
+            parts.at[kind, b, r, 1 - core], core_in.at[kind, b, r], core_send.at[kind, b, r],
+            core_recv.at[kind, b, r], {"heads": head + 1 - 2 * core},
+        )
+
+    def round_partial(b, r, slot, kind=0):
         for k in range(cores):
-            parts[kind, b, k] = acc[slot, :, k * half : (k + 1) * half].astype(BF)
-        core_copy(b, kind).start()
-
-    def chip_copy(b, k, kind):
+            parts[kind, b, r, k] = acc[slot, r, :, k * half : (k + 1) * half].astype(BF)
+        core_copy(b, r, kind).start()
+
+    def chip_copy(b, r, k, kind):
         to = (chip + k) % chips
         return remote(
-            chip_out.at[kind, b, to], x_in.at[kind, b, k], x_send.at[kind, b, k],
-            x_recv.at[kind, b, k], {"heads": to * cores + core},
-        )
-
-    def sum_cores(b, kind=0):
-        core_copy(b, kind).wait_recv()
+            chip_out.at[kind, b, r, to], x_in.at[kind, b, r, k], x_send.at[kind, b, r, k],
+            x_recv.at[kind, b, r, k], {"heads": to * cores + core},
+        )
+
+    def sum_cores(b, r, kind=0):
+        core_copy(b, r, kind).wait_recv()
         for k in range(chips):
             part = slice(k * strip, (k + 1) * strip)
-            both = parts[kind, b, core, part].astype(F32) + core_in[kind, b, part].astype(F32)
-            chip_out[kind, b, k] = both.astype(BF)
+            both = parts[kind, b, r, core, part].astype(F32) + core_in[kind, b, r, part].astype(F32)
+            chip_out[kind, b, r, k] = both.astype(BF)
         for k in range(1, chips):
-            chip_copy(b, k, kind).start()
+            chip_copy(b, r, k, kind).start()
 
     def local_final(b, column):
         return jnp.logical_and(b == me, head == column // share)
 
-    def final_copy(b, column, kind):
-        return remote(
-            fin_out.at[kind, b], final.at[column % share, head], fin_send.at[kind, b],
-            fin_recv.at[column % share, head], {"ctx": b, "heads": column // share},
-        )
-
-    def strip_copy(b):
-        return remote(
-            fin_out.at[0, b], strips.at[b], fin_send.at[0, b], strip_recv.at[b],
+    def final_copy(b, r, column, kind):
+        return remote(
+            fin_out.at[kind, b, r], final.at[column % share, head, r], fin_send.at[kind, b, r],
+            fin_recv.at[column % share, head, r], {"ctx": b, "heads": column // share},
+        )
+
+    def strip_copy(b, r):
+        return remote(
+            fin_out.at[0, b, r], strips.at[b, r], fin_send.at[0, b, r], strip_recv.at[b, r],
             {"ctx": beside_here},
         )
 
@@ -328,63 +353,63 @@
             return False
         return jnp.logical_and(at_end, b != me)
 
-    def strip_total(b, kind):
+    def strip_total(b, r, kind):
         part = pl.ds(pl.multiple_of(chip * strip, strip), strip)
-        total = parts[kind, b, core, part].astype(F32) + core_in[kind, b, part].astype(F32)
+        total = parts[kind, b, r, core, part].astype(F32) + core_in[kind, b, r, part].astype(F32)
         for k in range(1, chips):
-            chip_copy(b, k, kind).wait_recv()
-            total = total + x_in[kind, b, k].astype(F32)
+            chip_copy(b, r, k, kind).wait_recv()
+            total = total + x_in[kind, b, r, k].astype(F32)
         return total
 
-    def deliver(b, column, kind, total):
+    def deliver(b, r, column, kind, total):
         @pl.when(local_final(b, column))
         def _():
-            final[column % share, head] = total.astype(BF)
+            final[column % share, head, r] = total.astype(BF)
 
         pl.when(jnp.logical_not(local_final(b, column)))(
-            lambda: final_copy(b, column, kind).start()
-        )
-
-    def sum_chips(b):
-        total = strip_total(b, 0)
-        fin_out[0, b] = total.astype(BF)
+            lambda: final_copy(b, r, column, kind).start()
+        )
+
+    def sum_chips(b, r):
+        total = strip_total(b, r, 0)
+        fin_out[0, b, r] = total.astype(BF)
         if lent:
-            pl.when(to_beside(b))(lambda: strip_copy(b).start())
-            pl.when(jnp.logical_not(to_beside(b)))(lambda: deliver(b, me, 0, total))
+            pl.when(to_beside(b))(lambda: strip_copy(b, r).start())
+            pl.when(jnp.logical_not(to_beside(b)))(lambda: deliver(b, r, me, 0, total))
         else:
-            deliver(b, me, 0, total)
+            deliver(b, r, me, 0, total)
 
     def helps(b):
         return jnp.logical_and(beside, b != end_here)
 
-    def helping(b):
+    def helping(b, r):
         @pl.when(helps(b))
         def _():
-            step = min(out_width, 256)
-            for lo in range(0, out_width, step):
-                total = jnp.zeros((rows, step), F32)
-                for k in range(lent):
-                    part = borrowed[k * piece : (k + 1) * piece, lo : lo + step]
-                    total = total + jnp.dot(
-                        blocks[b, keep + k], part, preferred_element_type=F32
-                    )
-                acc[2, :, lo : lo + step] = total
-            round_partial(b, 2, 1)
-
-    def combine(b):
+            for lo in range(0, out_width, col_step):
+                acc[2, r, :, lo : lo + col_step] = jnp.dot(
+                    rest[b, r], borrowed[:, lo : lo + col_step], preferred_element_type=F32
+                )
+            round_partial(b, r, 2, 1)
+
+    def reduce_help(b, r):
+        pl.when(helps(b))(lambda: sum_cores(b, r, 1))
+
+    def combine(b, r):
         @pl.when(helps(b))
         def _():
-            strip_copy(b).wait_recv()
-            total = strip_total(b, 1) + strips[b].astype(F32)
-            fin_out[1, b] = total.astype(BF)
-            deliver(b, end_here, 1, total)
-
-    def own(p, carry):
-        multiply(0, me, p)
+            strip_copy(b, r).wait_recv()
+            total = strip_total(b, r, 1) + strips[b, r].astype(F32)
+            fin_out[1, b, r] = total.astype(BF)
+            deliver(b, r, end_here, 1, total)
+
+    def own(r, carry):
+        multiply(0, me, r)
+        if lent:
+            multiply_rest(0, me, r)
+        round_partial(me, r, 0)
         return carry
 
-    lax.fori_loop(0, count, own, 0)
-    round_partial(me, 0)
+    lax.fori_loop(0, waves, own, 0)
 
     loads[9].wait()
     loads[10].wait()
@@ -403,71 +428,117 @@
         placed[part] = jnp.where(here, 1.0, 0.0).astype(BF)
         table[part] = jnp.where(here, weight, 0.0).astype(BF)
 
+    held_back = jnp.where(me == 1, 1, 0) if lent else 0
+
+    def low_block(s):
+        low = me - s + jnp.where(s > 0, held_back, 0)
+        return jnp.where(jnp.logical_and(s > 0, low >= me), -1, low)
+
     def around(s, act):
-        low, high = me - s, me + s
+        low, high = low_block(s), me + s
         pl.when(low >= 0)(lambda: act(jnp.maximum(low, 0), 0))
 
         @pl.when(jnp.logical_and(high < n, s > 0))
         def _():
             act(jnp.minimum(high, n - 1), 1)
 
-    def both_sides(s, act):
-        around(s, lambda b, slot: act(b))
+    turns = 2 * waves
+    ripe = jnp.where(at_end, 0, waves) if lent else 0
+
+    def finished(i, act):
+        s, r = i // turns, i % turns - ripe
+        fits = jnp.logical_and(jnp.logical_and(r >= 0, r < waves), s > 0)
+        spot = jnp.maximum(jnp.minimum(r, waves - 1), 0)
+        pl.when(fits)(lambda: around(s, lambda b, slot: act(b, spot, slot)))
+
+    def pass_on(k):
+        lend(k).wait_recv()
+        for g in range(1, groups):
+            spread(k, g).start()
+
+    for r in range(waves):
+        sum_cores(me, r)
+    for r in range(waves):
+        sum_chips(me, r)
+    for k in range(lent):
+        pl.when(me == n - 2)(lambda: pass_on(k))
+    first_help = 2 * turns + waves
 
     def step(i, carry):
-        s, p = 1 + i // count, i % count
-        low, high = me - s, me + s
+        s, u = i // turns, i % turns
+        low, high = low_block(s), me + s
         low_spot, high_spot = jnp.maximum(low, 0), jnp.minimum(high, n - 1)
-        wanted = needed(p)
-
-        @pl.when(jnp.logical_and(low >= 0, wanted))
+        has_low, has_high = low >= 0, high < n
+
+        @pl.when(u < waves)
         def _():
-            upward(low_spot, p).wait_recv()
-            pl.when(goes_up(p))(lambda: upward(low_spot, p).start())
-
-        @pl.when(jnp.logical_and(high < n, wanted))
-        def _():
-            downward(high_spot, p).wait_recv()
-            pl.when(goes_down(p))(lambda: downward(high_spot, p).start())
-
-        pl.when(wanted)(lambda: around(s, lambda b, slot: multiply(slot, b, p)))
-        last = jnp.where(at_end, keep - 1, count - 1)
-        pl.when(p == last)(lambda: around(s, round_partial))
-
-        def at(spot, act):
-            pl.when(p == min(spot, count - 1))(lambda: both_sides(s - 1, act))
-
-        at(1, sum_cores)
-        at(4, sum_chips)
-        def reduce_help(b):
-            pl.when(helps(b))(lambda: sum_cores(b, 1))
+            r = jnp.minimum(u, waves - 1)
+
+            @pl.when(has_low)
+            def _():
+                upward(low_spot, r).wait_recv()
+                pl.when(has_next)(lambda: upward(low_spot, r).start())
+
+            @pl.when(has_high)
+            def _():
+                downward(high_spot, r).wait_recv()
+                pl.when(has_prev)(lambda: downward(high_spot, r).start())
+
+            around(s, lambda b, slot: multiply(slot, b, r))
 
         if lent:
-            @pl.when(jnp.logical_and(i == 1, beside))
+            @pl.when(jnp.logical_and(u >= waves, inner))
+            def _():
+                r = jnp.maximum(u - waves, 0)
+
+                @pl.when(has_low)
+                def _():
+                    upward_rest(low_spot, r).wait_recv()
+                    pl.when(rest_up)(lambda: upward_rest(low_spot, r).start())
+
+                @pl.when(has_high)
+                def _():
+                    downward_rest(high_spot, r).wait_recv()
+                    pl.when(rest_down)(lambda: downward_rest(high_spot, r).start())
+
+                around(s, lambda b, slot: multiply_rest(slot, b, r))
+
+        finished(i, lambda b, r, slot: round_partial(b, r, slot))
+        finished(i - 1, lambda b, r, slot: sum_cores(b, r))
+        finished(i - 3, lambda b, r, slot: sum_chips(b, r))
+        for k in range(lent):
+            when = min(turns + waves + (k + 1) * waves // lent, 2 * turns)
+            pl.when(jnp.logical_and(i == when, me == 1))(lambda: pass_on(k))
+        if lent:
+            def early_help(spot, act):
+                r = jnp.maximum(jnp.minimum(i - spot, waves - 1), 0)
+
+                @pl.when(jnp.logical_and(i >= spot, i < spot + waves))
+                def _():
+                    for base in range(2):
+                        around(base, lambda b, slot: act(b, r))
+
+            @pl.when(jnp.logical_and(i == first_help, beside))
             def _():
                 for k in range(lent):
                     for g in range(1, groups):
                         spread(k, g, True).wait_recv()
 
-            at(2, helping)
-            at(4, reduce_help)
-            pl.when(jnp.logical_and(p == min(7, count - 1), s > 1))(
-                lambda: both_sides(s - 2, combine)
-            )
+            early_help(first_help, helping)
+            early_help(first_help + 1, reduce_help)
+            early_help(first_help + 4, combine)
+
+            def later(back, act):
+                pl.when(i - back >= 2 * turns)(
+                    lambda: finished(i - back, lambda b, r, slot: act(b, r))
+                )
+
+            later(1, helping)
+            later(2, reduce_help)
+            later(4, combine)
         return carry
 
-    for k in range(lent):
-        @pl.when(beside)
-        def _():
-            lend(k).wait_recv()
-            for g in range(1, groups):
-                spread(k, g).start()
-
-    lax.fori_loop(0, (n - 1) * count, step, 0)
-    both_sides(n - 1, sum_cores)
-    both_sides(n - 1, sum_chips)
-    if lent:
-        both_sides(n - 2, combine)
+    lax.fori_loop(turns, n * turns + 4, step, 0)
     loads[8].wait()
 
     for j in range(share):
@@ -478,18 +549,20 @@
         for k in range(heads):
             here = jnp.logical_and(source == me, k == head)
 
-            @pl.when(jnp.logical_not(here))
-            def _():
-                remote(
-                    fin_out.at[0, 0], final.at[j, k], fin_send.at[0, 0], fin_recv.at[j, k],
-                    {"ctx": source, "heads": k},
-                ).wait_recv()
-
-            part = slice((k // cores) * strip, (k // cores + 1) * strip)
-            lo = j * out_width + (k % cores) * half
-            residual[part, lo : lo + half] = (
-                resid_ref[part, lo : lo + half].astype(F32) + final[j, k].astype(F32)
-            )
+            for r in range(waves):
+                @pl.when(jnp.logical_not(here))
+                def _():
+                    remote(
+                        fin_out.at[0, 0, r], final.at[j, k, r], fin_send.at[0, 0, r],
+                        fin_recv.at[j, k, r], {"ctx": source, "heads": k},
+                    ).wait_recv()
+
+                base = r * band_rows + (k // cores) * strip
+                part = slice(base, base + strip)
+                lo = j * out_width + (k % cores) * half
+                residual[part, lo : lo + half] = (
+                    resid_ref[part, lo : lo + half].astype(F32) + final[j, k, r].astype(F32)
+                )
 
     for load in loads[11:]:
         load.wait()
@@ -653,24 +726,28 @@
     for q in range(pairs):
         pl.when(has_next)(lambda: chain_copy(q).wait_send())
     for b in range(n):
-        for p in range(count):
-            pl.when(jnp.logical_and(goes_up(p), b <= me))(lambda: upward(b, p).wait_send())
-            pl.when(jnp.logical_and(goes_down(p), b >= me))(lambda: downward(b, p).wait_send())
-        core_copy(b, 0).wait_send()
-        for k in range(1, chips):
-            chip_copy(b, k, 0).wait_send()
         sent = jnp.logical_or(to_beside(b), jnp.logical_not(local_final(b, me)))
-        pl.when(sent)(lambda: final_copy(b, me, 0).wait_send())
-
-        if lent:
-            @pl.when(helps(b))
-            def _():
-                core_copy(b, 1).wait_send()
-                for k in range(1, chips):
-                    chip_copy(b, k, 1).wait_send()
-                pl.when(jnp.logical_not(local_final(b, end_here)))(
-                    lambda: final_copy(b, end_here, 1).wait_send()
+        for r in range(waves):
+            pl.when(jnp.logical_and(has_next, b <= me))(lambda: upward(b, r).wait_send())
+            pl.when(jnp.logical_and(has_prev, b >= me))(lambda: downward(b, r).wait_send())
+            core_copy(b, r, 0).wait_send()
+            for k in range(1, chips):
+                chip_copy(b, r, k, 0).wait_send()
+            pl.when(sent)(lambda: final_copy(b, r, me, 0).wait_send())
+            if lent:
+                pl.when(jnp.logical_and(rest_up, b <= me))(lambda: upward_rest(b, r).wait_send())
+                pl.when(jnp.logical_and(rest_down, b >= me))(
+                    lambda: downward_rest(b, r).wait_send()
                 )
+
+                @pl.when(helps(b))
+                def _():
+                    core_copy(b, r, 1).wait_send()
+                    for k in range(1, chips):
+                        chip_copy(b, r, k, 1).wait_send()
+                    pl.when(jnp.logical_not(local_final(b, end_here)))(
+                        lambda: final_copy(b, r, end_here, 1).wait_send()
+                    )
 
     for k in range(lent):
         pl.when(at_end)(lambda: lend(k).wait_send())
@@ -719,9 +796,10 @@
     out_width = weight.shape[1]
     share = n // heads
     chips = heads // 2
-    half, strip = out_width // 2, rows // chips
+    half, band_rows = out_width // 2, rows // WAVES
+    strip = band_rows // chips
+    keep_width, rest_width = (count - lent) * piece, max(lent, 1) * piece
     lane_count = -(-head_count // 128) * 128
-    block = (rows, out_width)
     features = residual_in.shape[1]
     experts_here = expert_up.shape[0]
     wave = experts_here * n
@@ -731,7 +809,7 @@
     ids, fixed = expert_ids.T, combine_fixed.T
     anywhere = pl.BlockSpec(memory_space=pltpu.HBM)
     return pl.pallas_call(
-        functools.partial(layer_kernel, n, heads, groups, width, piece, 3, lent),
+        functools.partial(layer_kernel, n, heads, groups, width, piece, 3, lent, WAVES),
         out_shape=jax.ShapeDtypeStruct((rows, features), BF),
         in_specs=[anywhere] * 16,
         out_specs=vmem()[0],
@@ -762,16 +840,17 @@
             pltpu.VMEM((pairs, states, span), BF),
             pltpu.VMEM((pairs, states, span), BF),
             pltpu.VMEM((GRP // span, rows, span), F32),
-            pltpu.VMEM((n, count, rows, piece), BF),
-            pltpu.VMEM((3,) + block, F32),
-            pltpu.VMEM((2, n, 2, rows, half), BF),
-            pltpu.VMEM((2, n, rows, half), BF),
-            pltpu.VMEM((2, n, chips, strip, half), BF),
-            pltpu.VMEM((2, n, chips, strip, half), BF),
-            pltpu.VMEM((2, n, strip, half), BF),
-            pltpu.VMEM((share, heads, strip, half), BF),
-            pltpu.VMEM((max(lent, 1) * piece, out_width), BF),
-            pltpu.VMEM((n, strip, half), BF),
+            pltpu.VMEM((n, WAVES, band_rows, keep_width), BF),
+            pltpu.VMEM((n, WAVES, band_rows, rest_width), BF),
+            pltpu.VMEM((3, WAVES, band_rows, out_width), F32),
+            pltpu.VMEM((2, n, WAVES, 2, band_rows, half), BF),
+            pltpu.VMEM((2, n, WAVES, band_rows, half), BF),
+            pltpu.VMEM((2, n, WAVES, chips, strip, half), BF),
+            pltpu.VMEM((2, n, WAVES, chips, strip, half), BF),
+            pltpu.VMEM((2, n, WAVES, strip, half), BF),
+            pltpu.VMEM((share, heads, WAVES, strip, half), BF),
+            pltpu.VMEM((rest_width, out_width), BF),
+            pltpu.VMEM((n, WAVES, strip, half), BF),
             pltpu.VMEM((rows, features), F32),
             pltpu.VMEM((wave, rows), F32),
             pltpu.VMEM((wave, rows), jnp.int32),
@@ -788,9 +867,10 @@
             pltpu.VMEM((experts_here, n, CAP, strand), BF),
             pltpu.VMEM((heads, n, experts_here, CAP, strand), BF),
             dma(16), dma(pairs), dma(pairs),
-            dma(n, count), dma(n, count), dma(n, count), dma(n, count),
-            dma(2, n), dma(2, n), dma(2, n, chips), dma(2, n, chips), dma(2, n), dma(share, heads),
-            dma(max(lent, 1)), dma(max(lent, 1)), dma(max(lent, 1), groups), dma(max(lent, 1), groups), dma(n),
+            *[dma(n, WAVES)] * 8,
+            dma(2, n, WAVES), dma(2, n, WAVES), dma(2, n, WAVES, chips), dma(2, n, WAVES, chips),
+            dma(2, n, WAVES), dma(share, heads, WAVES),
+            dma(max(lent, 1)), dma(max(lent, 1)), dma(max(lent, 1), groups), dma(max(lent, 1), groups), dma(n, WAVES),
             dma(heads), dma(heads), dma(heads), dma(heads), dma(n), dma(n),
             dma(n, heads), dma(n, heads), dma(experts_here, heads), dma(experts_here, heads),
             dma(experts_here, n), dma(experts_here, n), dma(n, heads), dma(n, heads),

time: 127 us -> 120 us (0.945)
  Pallas kernels: 124 us -> 118 us
    pallas_call x1, Pallas kernels: 124 us -> 118 us  [local(): pl.pallas_call(functools.partial(layer_kernel, n, heads, groups, width, p...]
where the time goes in v6:
time: 120 us
  Pallas kernels  118 us (98%)
  local copies, waits for them, and re-layouts  1.87 us (2%)
    pallas_call x1, Pallas kernels, local(): pl.pallas_call(functools.partial(layer_kernel, n, heads, groups, width, p...  118 us

profile of v6, /device:TPU:1, one launch (start us, length us, event | category | flops | bytes accessed | tf_op | source)
XLA Modules:
  0.0 119.6 jit_solution(5864663613003057430)
XLA Ops:
  0.0 117.7 %shard_map.154 = bf16[256,1024]{1,0:T(8,128)(2,1)} custom-call(bf16[256,2048]{1,0:T(8,128)(2,1)} %x_hbm.1, bf16[256,128]{1,0:T(8,128)(2,1)} %write_hbm.1, bf16[256,128]{1,0:T(8,128)(2,1)} %read_hbm.1, f32[32,256]{1,0:T(8,128)} %bitcast.8, f32[1,32]{1,0:T(1,128)} %bitcast.13, bf16[2048,1024]{1,0:T(8,128)(2,1)} %weight_hbm.1, bf16[256,2048]{1,0:T(8,128)(2,1)} %gate_hbm.1, ...), custom_call_target="tpu_custom_call" | custom-call | tf_op jit(solution)/shard_map/pallas_call | solution.py:811
  117.7 1.9 %copy.18 = bf16[256,1024]{1,0:T(8,128)(2,1)} copy(bf16[256,1024]{1,0:T(8,128)(2,1)} %shard_map.154) | data formatting | bytes 1048576

commit v7 on v6

--- a/solution.py
+++ b/solution.py
@@ -424,7 +424,8 @@
     for e in range(wave):
         here = jnp.logical_and(chosen[e : e + 1, :] > 0.5, taken[e : e + 1, :] == slot)
         weight = weights[e : e + 1, :].astype(F32) / 65536.0
-        part = slice(e * CAP, (e + 1) * CAP)
+        base = (e % grow_ref.shape[0] * n + e // grow_ref.shape[0]) * CAP
+        part = slice(base, base + CAP)
         placed[part] = jnp.where(here, 1.0, 0.0).astype(BF)
         table[part] = jnp.where(here, weight, 0.0).astype(BF)
 
@@ -570,16 +571,10 @@
     strand = latent_width // heads
     features = residual.shape[1] * heads
     experts_here = grow_ref.shape[0]
-    slot_rows = experts_here * CAP
+    slot_rows = n * CAP
     held = residual[...]
     scaled = (held * moe_ref[...]).astype(BF)
     picked = jnp.dot(placed[...], scaled, preferred_element_type=F32).astype(BF)
-    power = jnp.sum(held * held, axis=1, keepdims=True)
-    power = jnp.transpose(jnp.broadcast_to(power, (rows, 128)))[:8, :]
-    square_out[...] = lax.dot_general(
-        power, placed[...].astype(F32), (((1,), (1,)), ((), ())),
-        precision=lax.Precision.HIGHEST, preferred_element_type=F32,
-    )
 
     def square_copy(k):
         return remote(
@@ -587,34 +582,63 @@
             {"heads": (head + k) % heads},
         )
 
-    def first_copy(k):
-        to = (head + k) % heads
-        return remote(
-            slots_out.at[k], slots_in.at[k], first_send.at[k], first_recv.at[k], {"heads": to}
-        )
-
-    for k in range(1, heads):
-        square_copy(k).start()
-    for k in [*range(1, heads), 0]:
-        to = (head + k) % heads
-        lane = pl.ds(pl.multiple_of(to * strand, strand), strand)
-        value = jnp.dot(picked, latent_ref[:, lane], preferred_element_type=F32).astype(BF)
-        for z in range(n):
-            slots_out[k, z] = value[z * slot_rows : (z + 1) * slot_rows]
-        if k:
-            first_copy(k).start()
-
-    def second_copy(k):
+    def first_copy(e, k):
+        return remote(
+            slots_out.at[e, k], slots_in.at[e, k], first_send.at[e, k], first_recv.at[e, k],
+            {"heads": (head + k) % heads},
+        )
+
+    def second_copy(e, k):
         to = (me + k) % n
         return remote(
-            middle.at[to], gathered.at[head, me], second_send.at[k], second_recv.at[k], {"ctx": to}
-        )
-
-    def third_copy(k, j):
-        spot = gathered.at[head, (me + n - k) % n]
-        return remote(
-            spot, spot, third_send.at[k, j], third_recv.at[k, j], {"heads": (head + j) % heads}
-        )
+            middle.at[e, to], gathered.at[e, head, me], second_send.at[e, k],
+            second_recv.at[e, k], {"ctx": to},
+        )
+
+    def third_copy(e, j):
+        spot = gathered.at[e, head]
+        return remote(
+            spot, spot, third_send.at[e, j], third_recv.at[e, j], {"heads": (head + j) % heads}
+        )
+
+    def fourth_copy(e, k):
+        return remote(
+            back_out.at[e, (head + k) % heads], back_in.at[e, k], fourth_send.at[e, k],
+            fourth_recv.at[e, k], {"heads": (head + k) % heads},
+        )
+
+    def fifth_copy(e, k):
+        to = (me + k) % n
+        return remote(
+            back_middle.at[e, to], returned.at[head, e, me], fifth_send.at[e, k],
+            fifth_recv.at[e, k], {"ctx": to},
+        )
+
+    def sixth_copy(e, j):
+        spot = returned.at[head, e]
+        return remote(
+            spot, spot, sixth_send.at[e, j], sixth_recv.at[e, j], {"heads": (head + j) % heads}
+        )
+
+    far = heads // 2
+    for e in range(experts_here):
+        rows_here = picked[e * slot_rows : (e + 1) * slot_rows]
+        for k in [far] + [k for k in range(1, heads) if k != far] + [0]:
+            to = (head + k) % heads
+            lane = pl.ds(pl.multiple_of(to * strand, strand), strand)
+            value = jnp.dot(rows_here, latent_ref[:, lane], preferred_element_type=F32)
+            slots_out[e, k] = value.astype(BF).reshape(n, CAP, strand)
+            if k:
+                first_copy(e, k).start()
+        if e == 0:
+            power = jnp.sum(held * held, axis=1, keepdims=True)
+            power = jnp.transpose(jnp.broadcast_to(power, (rows, 128)))[:8, :]
+            square_out[...] = lax.dot_general(
+                power, placed[...].astype(F32), (((1,), (1,)), ((), ())),
+                precision=lax.Precision.HIGHEST, preferred_element_type=F32,
+            )
+            for k in range(1, heads):
+                square_copy(k).start()
 
     power = square_out[...]
     for k in range(1, heads):
@@ -622,48 +646,28 @@
         power = power + square_in[k]
     scale = lax.rsqrt(power / features + epsilon)
     scale = jnp.transpose(jnp.broadcast_to(scale[0:1, :], (128, scale.shape[1])))
-    for k in range(1, heads):
-        first_copy(k).wait_recv()
-    for z in range(n):
-        total = slots_out[0, z].astype(F32)
+    for e in range(experts_here):
         for k in range(1, heads):
-            total = total + slots_in[k, z].astype(F32)
-        middle[z] = (total * scale[z * slot_rows : (z + 1) * slot_rows, 0:1]).astype(BF)
-    for k in range(1, n):
-        second_copy(k).start()
-    gathered[head, me] = middle[me]
-    for k in range(n):
-        if k:
-            second_copy(k).wait_recv()
+            first_copy(e, k).wait_recv()
+        for z in range(n):
+            total = slots_out[e, 0, z].astype(F32)
+            for k in range(1, heads):
+                total = total + slots_in[e, k, z].astype(F32)
+            base = e * slot_rows + z * CAP
+            middle[e, z] = (total * scale[base : base + CAP, 0:1]).astype(BF)
+        for k in range(1, n):
+            second_copy(e, k).start()
+        gathered[e, head, me] = middle[e, me]
+    for e in range(experts_here):
+        for k in range(1, n):
+            second_copy(e, k).wait_recv()
         for j in range(1, heads):
-            third_copy(k, j).start()
-    for k in range(n):
+            third_copy(e, j).start()
+    for e in range(experts_here):
         for j in range(1, heads):
-            third_copy(k, j).wait_recv()
-
-    def fourth_copy(e, k):
-        return remote(
-            back_out.at[e, (head + k) % heads], back_in.at[e, k], fourth_send.at[e, k],
-            fourth_recv.at[e, k], {"heads": (head + k) % heads},
-        )
-
-    def fifth_copy(e, k):
-        to = (me + k) % n
-        return remote(
-            back_middle.at[e, to], returned.at[head, me, e], fifth_send.at[e, k],
-            fifth_recv.at[e, k], {"ctx": to},
-        )
-
-    def sixth_copy(k, j):
-        spot = returned.at[head, (me + n - k) % n]
-        return remote(
-            spot, spot, sixth_send.at[k, j], sixth_recv.at[k, j], {"heads": (head + j) % heads}
-        )
-
-    for e in range(experts_here):
-        part = slice(e * CAP, (e + 1) * CAP)
+            third_copy(e, j).wait_recv()
         fed = jnp.concatenate(
-            [gathered[h, :, part].reshape(n * CAP, strand) for h in range(heads)], axis=1
+            [gathered[e, h].reshape(slot_rows, strand) for h in range(heads)], axis=1
         )
         hidden = lax.dot_general(
             fed, grow_ref[e], (((1,), (1,)), ((), ())), preferred_element_type=F32
@@ -671,8 +675,7 @@
         hidden = (jnp.maximum(hidden, 0.0) ** 2).astype(BF)
         value = jnp.dot(hidden, shrink_ref[e], preferred_element_type=F32).astype(BF)
         for h in range(heads):
-            for z in range(n):
-                back_out[e, h, z] = value[z * CAP : (z + 1) * CAP, h * strand : (h + 1) * strand]
+            back_out[e, h] = value[:, h * strand : (h + 1) * strand].reshape(n, CAP, strand)
         for k in range(1, heads):
             fourth_copy(e, k).start()
     for e in range(experts_here):
@@ -684,16 +687,15 @@
         back_middle[e] = total.astype(BF)
         for k in range(1, n):
             fifth_copy(e, k).start()
-        returned[head, me, e] = back_middle[e, me]
-    for k in range(n):
-        if k:
-            for e in range(experts_here):
-                fifth_copy(e, k).wait_recv()
+        returned[head, e, me] = back_middle[e, me]
+    for e in range(experts_here):
+        for k in range(1, n):
+            fifth_copy(e, k).wait_recv()
         for j in range(1, heads):
-            sixth_copy(k, j).start()
-    for k in range(n):
+            sixth_copy(e, j).start()
+    for e in range(experts_here):
         for j in range(1, heads):
-            sixth_copy(k, j).wait_recv()
+            sixth_copy(e, j).wait_recv()
     combined = jnp.concatenate(
         [
             lax.dot_general(
@@ -712,17 +714,15 @@
 
     for k in range(1, heads):
         square_copy(k).wait_send()
-        first_copy(k).wait_send()
-        for e in range(experts_here):
+    for e in range(experts_here):
+        for k in range(1, heads):
+            first_copy(e, k).wait_send()
+            third_copy(e, k).wait_send()
             fourth_copy(e, k).wait_send()
-    for k in range(n):
-        for j in range(1, heads):
-            third_copy(k, j).wait_send()
-            sixth_copy(k, j).wait_send()
-        if k:
-            second_copy(k).wait_send()
-            for e in range(experts_here):
-                fifth_copy(e, k).wait_send()
+            sixth_copy(e, k).wait_send()
+        for k in range(1, n):
+            second_copy(e, k).wait_send()
+            fifth_copy(e, k).wait_send()
     for q in range(pairs):
         pl.when(has_next)(lambda: chain_copy(q).wait_send())
     for b in range(n):
@@ -803,13 +803,12 @@
     features = residual_in.shape[1]
     experts_here = expert_up.shape[0]
     wave = experts_here * n
-    slot_rows = experts_here * CAP
     strand = down_latent.shape[1] // heads
     grow = expert_up.transpose(0, 2, 1)
     ids, fixed = expert_ids.T, combine_fixed.T
     anywhere = pl.BlockSpec(memory_space=pltpu.HBM)
     return pl.pallas_call(
-        functools.partial(layer_kernel, n, heads, groups, width, piece, 3, lent, WAVES),
+        functools.partial(layer_kernel, n, heads, groups, width, piece, 4, lent, WAVES),
         out_shape=jax.ShapeDtypeStruct((rows, features), BF),
         in_specs=[anywhere] * 16,
         out_specs=vmem()[0],
@@ -858,22 +857,23 @@
             pltpu.VMEM((wave * CAP, rows), BF),
             pltpu.VMEM((8, wave * CAP), F32),
             pltpu.VMEM((heads, 8, wave * CAP), F32),
-            pltpu.VMEM((heads, n, slot_rows, strand), BF),
-            pltpu.VMEM((heads, n, slot_rows, strand), BF),
-            pltpu.VMEM((n, slot_rows, strand), BF),
-            pltpu.VMEM((heads, n, slot_rows, strand), BF),
             pltpu.VMEM((experts_here, heads, n, CAP, strand), BF),
             pltpu.VMEM((experts_here, heads, n, CAP, strand), BF),
             pltpu.VMEM((experts_here, n, CAP, strand), BF),
-            pltpu.VMEM((heads, n, experts_here, CAP, strand), BF),
+            pltpu.VMEM((experts_here, heads, n, CAP, strand), BF),
+            pltpu.VMEM((experts_here, heads, n, CAP, strand), BF),
+            pltpu.VMEM((experts_here, heads, n, CAP, strand), BF),
+            pltpu.VMEM((experts_here, n, CAP, strand), BF),
+            pltpu.VMEM((heads, experts_here, n, CAP, strand), BF),
             dma(16), dma(pairs), dma(pairs),
             *[dma(n, WAVES)] * 8,
             dma(2, n, WAVES), dma(2, n, WAVES), dma(2, n, WAVES, chips), dma(2, n, WAVES, chips),
             dma(2, n, WAVES), dma(share, heads, WAVES),
             dma(max(lent, 1)), dma(max(lent, 1)), dma(max(lent, 1), groups), dma(max(lent, 1), groups), dma(n, WAVES),
-            dma(heads), dma(heads), dma(heads), dma(heads), dma(n), dma(n),
-            dma(n, heads), dma(n, heads), dma(experts_here, heads), dma(experts_here, heads),
-            dma(experts_here, n), dma(experts_here, n), dma(n, heads), dma(n, heads),
+            dma(heads), dma(heads),
+            *[dma(experts_here, heads)] * 2, *[dma(experts_here, n)] * 2,
+            *[dma(experts_here, heads)] * 4,
+            *[dma(experts_here, n)] * 2, *[dma(experts_here, heads)] * 2,
         ],
         compiler_params=reaching(1, 67043328),
     )(

time: 120 us -> 118 us (0.983)
  Pallas kernels: 118 us -> 116 us
    pallas_call x1, Pallas kernels: 118 us -> 116 us  [local(): pl.pallas_call(functools.partial(layer_kernel, n, heads, groups, width, p...]
where the time goes in v7:
time: 118 us
  Pallas kernels  116 us (98%)
  local copies, waits for them, and re-layouts  1.87 us (2%)
    pallas_call x1, Pallas kernels, local(): pl.pallas_call(functools.partial(layer_kernel, n, heads, groups, width, p...  116 us

profile of v7, /device:TPU:1, one launch (start us, length us, event | category | flops | bytes accessed | tf_op | source)
XLA Modules:
  0.0 117.7 jit_solution(12423201537043832183)
XLA Ops:
  0.0 115.8 %shard_map.154 = bf16[256,1024]{1,0:T(8,128)(2,1)} custom-call(bf16[256,2048]{1,0:T(8,128)(2,1)} %x_hbm.1, bf16[256,128]{1,0:T(8,128)(2,1)} %write_hbm.1, bf16[256,128]{1,0:T(8,128)(2,1)} %read_hbm.1, f32[32,256]{1,0:T(8,128)} %bitcast.8, f32[1,32]{1,0:T(1,128)} %bitcast.13, bf16[2048,1024]{1,0:T(8,128)(2,1)} %weight_hbm.1, bf16[256,2048]{1,0:T(8,128)(2,1)} %gate_hbm.1, ...), custom_call_target="tpu_custom_call" | custom-call | tf_op jit(solution)/shard_map/pallas_call | solution.py:810
  115.8 1.9 %copy.18 = bf16[256,1024]{1,0:T(8,128)(2,1)} copy(bf16[256,1024]{1,0:T(8,128)(2,1)} %shard_map.154) | data formatting | bytes 1048576

commit v8 on v7

--- a/solution.py
+++ b/solution.py
@@ -281,12 +281,17 @@
     pl.when(me < n - 1)(lambda: loads[5].wait())
     for k in range(lent):
         pl.when(me == 0)(lambda: lend(k).start())
+    def begin_up():
+        for r in range(waves):
+            pl.when(has_next)(lambda: upward(me, r).start())
+
+    if early:
+        begin_up()
     for g in range(early, columns // GRP):
         gate(g)
     if not early:
         begin_down()
-    for r in range(waves):
-        pl.when(has_next)(lambda: upward(me, r).start())
+        begin_up()
     if lent:
         for r in range(waves):
             pl.when(rest_up)(lambda: upward_rest(me, r).start())

time: 118 us -> 118 us (level)
  no operation moved by 1% of the time
where the time goes in v8:
time: 118 us
  Pallas kernels  116 us (98%)
  local copies, waits for them, and re-layouts  1.87 us (2%)
    pallas_call x1, Pallas kernels, local(): pl.pallas_call(functools.partial(layer_kernel, n, heads, groups, width, p...  116 us

profile of v8, /device:TPU:1, one launch (start us, length us, event | category | flops | bytes accessed | tf_op | source)
XLA Modules:
  0.0 117.7 jit_solution(621904593541809223)
XLA Ops:
  0.0 115.8 %shard_map.154 = bf16[256,1024]{1,0:T(8,128)(2,1)} custom-call(bf16[256,2048]{1,0:T(8,128)(2,1)} %x_hbm.1, bf16[256,128]{1,0:T(8,128)(2,1)} %write_hbm.1, bf16[256,128]{1,0:T(8,128)(2,1)} %read_hbm.1, f32[32,256]{1,0:T(8,128)} %bitcast.8, f32[1,32]{1,0:T(1,128)} %bitcast.13, bf16[2048,1024]{1,0:T(8,128)(2,1)} %weight_hbm.1, bf16[256,2048]{1,0:T(8,128)(2,1)} %gate_hbm.1, ...), custom_call_target="tpu_custom_call" | custom-call | tf_op jit(solution)/shard_map/pallas_call | solution.py:815
  115.8 1.9 %copy.18 = bf16[256,1024]{1,0:T(8,128)(2,1)} copy(bf16[256,1024]{1,0:T(8,128)(2,1)} %shard_map.154) | data formatting | bytes 1048576
